TPU v7x, 32 devices: a whole 2x2x4 slice. The times are simulated.
32 devices in a mesh: fsdp: 8 (over z, y), rep: 4 (over x, core).
Axes of the slice: x: 2, y: 2, z: 4, core: 2. Of those that a mesh axis runs over, the one named last changes fastest.
Arguments:
- hidden: bfloat16 [8192, 2048], P(('fsdp', 'rep')), may hold values from -6 to 6
- attn_gain: bfloat16 [2048], P(('fsdp', 'rep')), may hold values from 0.25 to 1.75
- w_query: bfloat16 [2048, 2048], P(('fsdp', 'rep')), as said below
- w_key: bfloat16 [2048, 512], P(('fsdp', 'rep')), as said below
- w_value: bfloat16 [2048, 512], P(('fsdp', 'rep')), may hold values from -0.125 to 0.125
- w_out: bfloat16 [2048, 2048], P(None, ('fsdp', 'rep')), may hold values from -0.125 to 0.125
Outputs:
- mixed: bfloat16 [8192, 2048], P(('fsdp', 'rep'))
Inputs may be any that keep to these rules, and one draw needn't show every extreme that they name: `w_query`: entries of order 2048^(-1/2). `w_key`: entries of order 2048^(-1/2) times a factor up to twenty.
All inputs are finite; a program needn't handle non-finite values.
Results may differ from a plain program's by a relative error of at most 0.012.
The roundings to bfloat16 on the way count: a program that leaves them out, or rounds other values in their place, can miss the bound.
Values may be sent and summed in bfloat16 or wider, within the bound.
A program may use at most 64 MiB of HBM per device.

v0:
```python
import functools

import jax
import jax.numpy as jnp
from jax import lax
from jax.experimental import pallas as pl
from jax.experimental.pallas import tpu as pltpu
from jax.sharding import PartitionSpec as P

HD = 64


rope_base = 500000.0
norm_eps = 1e-05


def rope_tables(tokens, head_dim):
    position = jnp.arange(tokens, dtype=jnp.float32)
    freq = rope_base ** (-(jnp.arange(head_dim // 2, dtype=jnp.float32) * 2.0) / head_dim)
    angle = position[:, None] * freq[None, :]
    cos_table = jnp.concatenate([jnp.cos(angle), jnp.cos(angle)], axis=-1)
    sin_table = jnp.concatenate([jnp.sin(angle), jnp.sin(angle)], axis=-1)
    return (cos_table, sin_table)


def rotate(tensor, cos_table, sin_table):
    half = tensor.shape[-1] // 2
    turned = jnp.concatenate([-tensor[..., half:], tensor[..., :half]], axis=-1)
    return tensor * cos_table + turned * sin_table


ORDERS = ((("x", "z", "y"), 2), (("y", "z", "x"), 2), (("z", "x", "y"), 1), (("z", "y", "x"), 1))
KERNEL_DEVICES = 64


def chip_grid(fsdp, rep):
    x_count = max(rep // 2, 1)
    return {"z": fsdp // x_count, "y": x_count, "x": x_count}


def column_parts(width):
    tiles = width // 128
    total = sum(weight for _, weight in ORDERS)
    cuts, seen = [0], 0
    for _, weight in ORDERS:
        seen += weight
        cuts.append((tiles * seen + total // 2) // total * 128)
    return [(order, cuts[i], cuts[i + 1] - cuts[i]) for i, (order, _) in enumerate(ORDERS)]


def gather_kernel(fsdp, rep, shard, out, send_sem, recv_sem, own_sem):
    grid = chip_grid(fsdp, rep)
    row, col = lax.axis_index("fsdp"), lax.axis_index("rep")
    here = {"z": row // grid["y"], "y": row % grid["y"], "x": col // 2}
    core = col % 2
    parts = column_parts(shard.shape[1])
    chips = fsdp * rep // 2

    def device(at, which):
        return (at["z"] * grid["y"] + at["y"], at["x"] * 2 + which)

    def slot_of(at, which):
        place = device(at, which)
        return place[0] * rep + place[1]

    def nearest(dim, step):
        p, n = here[dim], grid[dim]
        if n != 4:
            return (p + step) % n
        middle = jnp.where((p == 1) | (p == 2), 1, 0)
        high = step // 2
        low = step % 2
        low = low + middle * high * (1 - 2 * low)
        first = (1 - 2 * (p % 2)) * low
        return p + first + (2 - 4 * (p // 2)) * high

    def origin(step, order):
        found = {}
        for dim in order:
            found[dim] = nearest(dim, step % grid[dim])
            step = step // grid[dim]
        return found

    def steps_along(dim, start):
        p, n = here[dim], grid[dim]
        if n == 2:
            return [(1 - p, p == start)]
        return [(p + 1, (p >= start) & (p + 1 < n)), (p - 1, (p <= start) & (p >= 1))]

    def moves(order, at):
        found = []
        for i, dim in enumerate(order):
            for target, go in steps_along(dim, at[dim]):
                for later in order[i + 1 :]:
                    go = go & (here[later] == at[later])
                found.append((go, device({**here, dim: target}, core)))
        found.append((None, device(here, 1 - core)))
        return found

    def copy(source, slot, step, part, move, target):
        _, begin, size = parts[part]
        piece = source if source is shard else out.at[slot]
        return pltpu.make_async_remote_copy(
            src_ref=piece.at[:, pl.ds(begin, size)],
            dst_ref=out.at[slot, :, pl.ds(begin, size)],
            send_sem=send_sem.at[step, part, move],
            recv_sem=recv_sem.at[slot, part],
            device_id=target,
            device_id_type=pl.DeviceIdType.MESH,
        )

    def each_move(source, step, part, act):
        at = origin(step, parts[part][0])
        slot = slot_of(at, core)
        for move, (go, target) in enumerate(moves(parts[part][0], at)):
            if go is None:
                act(copy(source, slot, step, part, move, target))
            else:

                @pl.when(go)
                def _(move=move, target=target):
                    act(copy(source, slot, step, part, move, target))

    barrier = pltpu.get_barrier_semaphore()
    around = [(None, device(here, 1 - core))]
    for dim in ("z", "y", "x"):
        for target, go in steps_along(dim, here[dim]):
            around.append((go, device({**here, dim: target}, core)))
    count = 0
    for go, target in around:
        if go is None:
            pl.semaphore_signal(
                barrier, inc=1, device_id=target, device_id_type=pl.DeviceIdType.MESH
            )
            count = count + 1
        else:

            @pl.when(go)
            def _(target=target):
                pl.semaphore_signal(
                    barrier, inc=1, device_id=target, device_id_type=pl.DeviceIdType.MESH
                )

            count = count + jnp.where(go, 1, 0)
    pl.semaphore_wait(barrier, count)

    own = pltpu.make_async_copy(shard, out.at[slot_of(here, core)], own_sem)
    for part in range(len(parts)):
        each_move(shard, 0, part, lambda c: c.start())
    own.start()

    def forward(step, carry):
        for part in range(len(parts)):
            at = origin(step, parts[part][0])
            copy(out, slot_of(at, core), step, part, 0, device(here, 1 - core)).wait_recv()
            each_move(out, step, part, lambda c: c.start())
        return carry

    lax.fori_loop(1, chips, forward, 0)
    own.wait()

    def finish(step, carry):
        for part in range(len(parts)):
            at = origin(step, parts[part][0])
            copy(out, slot_of(at, 1 - core), step, part, 0, device(here, 1 - core)).wait_recv()
            each_move(out, step, part, lambda c: c.wait_send())
        return carry

    lax.fori_loop(0, chips, finish, 0)


def gather_rows(shard, fsdp, rep):
    rows, width = shard.shape
    grid = chip_grid(fsdp, rep)
    moves = 1 + sum(1 if n == 2 else 2 for n in grid.values())
    devices = fsdp * rep
    gathered = pl.pallas_call(
        functools.partial(gather_kernel, fsdp, rep),
        out_shape=jax.ShapeDtypeStruct((devices, rows, width), shard.dtype),
        in_specs=[pl.BlockSpec(memory_space=pltpu.VMEM)],
        out_specs=pl.BlockSpec(memory_space=pl.ANY),
        scratch_shapes=[
            pltpu.SemaphoreType.DMA((devices // 2, len(ORDERS), moves)),
            pltpu.SemaphoreType.DMA((devices, len(ORDERS))),
            pltpu.SemaphoreType.DMA,
        ],
        compiler_params=pltpu.CompilerParams(collective_id=0, has_side_effects=True),
        name="gather_rows",
    )(shard)
    return gathered.reshape(devices * rows, width)


def body(fsdp, rep, hidden, attn_gain, w_query, w_key, w_value, w_out):
    tokens = hidden.shape[0]
    head_dim = HD
    width_query = w_query.shape[1]
    width_kv = w_key.shape[1]
    kv_count = width_kv // head_dim
    group = width_query // width_kv
    x_float = hidden.astype(jnp.float32)
    inv_rms = lax.rsqrt(jnp.mean(x_float * x_float, axis=-1, keepdims=True) + norm_eps)
    width_rows = w_query.shape[0]
    packed = jnp.concatenate(
        [w_query, w_key, w_value, w_out.T, jnp.broadcast_to(attn_gain[:, None], (width_rows, 128))],
        axis=1,
    )
    x_count = rep // 2
    if rep % 2 == 0 and x_count > 1 and fsdp % x_count == 0 and fsdp * rep <= KERNEL_DEVICES:
        packed = gather_rows(packed, fsdp, rep)
    else:
        packed = lax.all_gather(packed, ("fsdp", "rep"), axis=0, tiled=True)
    cut_key = width_query
    cut_value = cut_key + width_kv
    cut_out = cut_value + width_kv
    cut_gain = cut_out + w_out.shape[0]
    query_piece = packed[:, :cut_key]
    key_piece = packed[:, cut_key:cut_value]
    value_piece = packed[:, cut_value:cut_out]
    out_piece = packed[:, cut_out:cut_gain]
    gain_piece = packed[:, cut_gain]
    normed = (x_float * inv_rms * gain_piece.astype(jnp.float32)[None, :]).astype(jnp.bfloat16)
    queries = jnp.dot(normed, query_piece, preferred_element_type=jnp.float32)
    keys_raw = jnp.dot(normed, key_piece, preferred_element_type=jnp.float32)
    values_raw = jnp.dot(normed, value_piece, preferred_element_type=jnp.float32)
    cos_table, sin_table = rope_tables(tokens, head_dim)
    queries = queries.reshape(tokens, kv_count, group, head_dim)
    keys_raw = keys_raw.reshape(tokens, kv_count, head_dim)
    values_bf = values_raw.reshape(tokens, kv_count, head_dim).astype(jnp.bfloat16)
    rope_queries = rotate(queries, cos_table[:, None, None, :], sin_table[:, None, None, :]).astype(
        jnp.bfloat16
    )
    rope_keys = rotate(keys_raw, cos_table[:, None, :], sin_table[:, None, :]).astype(jnp.bfloat16)
    scores = jnp.einsum(
        "qkgd,skd->kgqs", rope_queries, rope_keys, preferred_element_type=jnp.float32
    ) * head_dim ** (-0.5)
    causal = jnp.arange(tokens)[:, None] >= jnp.arange(tokens)[None, :]
    scores = jnp.where(causal[None, None, :, :], scores, -1e30)
    top = jnp.max(scores, axis=-1, keepdims=True)
    expo = jnp.exp(scores - top)
    probs = (expo / jnp.sum(expo, axis=-1, keepdims=True)).astype(jnp.bfloat16)
    context = jnp.einsum("kgqs,skd->qkgd", probs, values_bf, preferred_element_type=jnp.float32)
    context = context.reshape(tokens, width_query).astype(jnp.bfloat16)
    branch = lax.dot_general(
        context, out_piece, (((1,), (1,)), ((), ())), preferred_element_type=jnp.float32
    )
    return (x_float + branch).astype(jnp.bfloat16)


def solution(mesh):
    placed = (
        P(("fsdp", "rep"), None),
        P(("fsdp", "rep")),
        P(("fsdp", "rep"), None),
        P(("fsdp", "rep"), None),
        P(("fsdp", "rep"), None),
        P(None, ("fsdp", "rep")),
    )
    return jax.shard_map(
        functools.partial(body, mesh.shape["fsdp"], mesh.shape["rep"]),
        mesh=mesh,
        in_specs=placed,
        out_specs=P(("fsdp", "rep"), None),
        check_vma=False,
    )
```

profile of v0, /device:TPU:0, one launch (start us, length us, event | category | flops | bytes accessed | tf_op | source)
XLA Modules:
  0.0 129.1 jit_solution(567840886937116323)
XLA Ops:
  0.0 1.0 constant_dynamic-update-slice_fusion.3
  1.0 0.8 constant_dynamic-update-slice_fusion.2
  1.8 0.8 constant_dynamic-update-slice_fusion.1
  2.7 1.0 bitcast_dynamic-update-slice_fusion
  3.6 0.7 constant_dynamic-update-slice_fusion.shard
  4.4 0.0 copy-start
  4.4 0.8 copy-done
  5.2 92.4 %gather_rows.1 = bf16[32,64,5248]{2,1,0:T(8,128)(2,1)} custom-call(bf16[64,5248]{1,0:T(8,128)(2,1)} %copy-done), custom_call_target="tpu_custom_call" | custom-call | tf_op jit(solution)/shard_map/gather_rows/pallas_call | solution.py:177
  97.7 0.0 copy-start.1
  97.7 1.2 slice_convert_fusion
  98.9 0.3 copy.26
  99.2 0.0 copy-done.1
  99.2 0.3 fusion.15
  99.5 2.6 %fusion.18 = f32[256,512]{0,1:T(8,128)S(1)} fusion(bf16[2048,5248]{1,0:T(8,128)(2,1)} %bitcast.33, bf16[256,2048]{1,0:T(8,128)(2,1)S(1)} %copy-done.1, f32[2048]{0:T(1024)S(1)} %bitcast.42, f32[256]{0:T(256)S(1)} %add_rsqrt_fusion), kind=kOutput, calls=%fused_computation.20 | convolution fusion | flops 538968064 | bytes 3679232 | tf_op jit(solution)/shard_map/dot_general | solution.py:223
  102.2 7.0 %fusion.3 = f32[256,2048]{0,1:T(8,128)S(1)} fusion(bf16[2048,5248]{1,0:T(8,128)(2,1)} %bitcast.34, bf16[256,2048]{1,0:T(8,128)(2,1)S(1)} %copy-done.1, f32[2048]{0:T(1024)S(1)} %bitcast.43, f32[256]{0:T(256)S(1)} %add_rsqrt_fusion), kind=kOutput, calls=%fused_computation.3 | convolution fusion | flops 2149580800 | bytes 11543552 | tf_op jit(solution)/shard_map/dot_general | solution.py:222
  109.2 0.2 slice_negate_fusion
  109.4 0.2 fusion.39
  109.6 1.3 %fusion.28 = f32[8,256,256,4]{2,1,3,0:T(8,128)S(1)} fusion(f32[256,8,4,32]{0,3,2,1:T(8,128)S(1)} %get-tuple-element.6, f32[256,8,4,32]{0,3,2,1:T(8,128)S(1)} %get-tuple-element.5, f32[256,8,4,64]{0,3,2,1:T(8,128)S(1)} %bitcast.38, f32[256,64]{0,1:T(8,128)S(1)} %get-tuple-element.14, f32[256,64]{0,1:T(8,128)S(1)} %get-tuple-element.13, ...), kind=kOutput, calls=%fused_computation.29 | convolution fusion | flops 271712256 | bytes 13762560 | tf_op jit(solution)/shard_map/qkgd,skd->kgqs/dot_general | solution.py:233
  111.0 4.6 %fusion.46 = (f32[8,4,256]{2,1,0:T(4,128)S(1)}, f32[8,4,256,256]{2,3,1,0:T(8,128)}) fusion(f32[8,256,256,4]{2,1,3,0:T(8,128)S(1)} %fusion.28, pred[256,256]{0,1:T(8,128)(4,1)S(1)} %iota_compare_fusion), kind=kOutput, calls=%fused_computation.57 | output fusion | flops 12583167 | bytes 16875520 | tf_op jit(solution)/shard_map/sub | solution.py:239
  115.6 2.3 %fusion.25 = bf16[256,512]{1,0:T(8,128)(2,1)S(1)} fusion(bf16[2048,5248]{1,0:T(8,128)(2,1)} %bitcast.35, bf16[256,2048]{1,0:T(8,128)(2,1)S(1)} %copy-done.1, f32[2048]{0:T(1024)S(1)} %bitcast.44, f32[256]{0:T(256)S(1)} %add_rsqrt_fusion), kind=kOutput, calls=%fused_computation.28 | convolution fusion | flops 539099136 | bytes 3417088 | tf_op jit(solution)/shard_map/dot_general | solution.py:224
  117.9 0.1 copy.16
  118.0 4.3 %fusion.24 = bf16[8,64,4,256]{3,1,2,0:T(8,128)(2,1)S(1)} fusion(bf16[256,8,64,1]{0,2,3,1:T(8,128)(2,1)S(1)} %bitcast.41, f32[8,4,256,256]{2,3,1,0:T(8,128)} %get-tuple-element.12, f32[8,4,256]{2,1,0:T(4,128)S(1)} %get-tuple-element.11), kind=kOutput, calls=%fused_computation.27 | convolution fusion | flops 273154048 | bytes 9732096 | tf_op jit(solution)/shard_map/kgqs,skd->qkgd/dot_general | solution.py:241
  122.3 6.8 %fusion.12 = bf16[256,2048]{1,0:T(8,128)(2,1)} fusion(bf16[256,2048]{0,1:T(8,128)(2,1)S(1)} %bitcast.45, bf16[2048,5248]{1,0:T(8,128)(2,1)} %bitcast.36, bf16[256,2048]{1,0:T(8,128)(2,1)S(1)} %copy-done.1), kind=kOutput, calls=%fused_computation.16 | convolution fusion | flops 2149056512 | bytes 11534336 | tf_op jit(solution)/shard_map/dot_general | solution.py:243
  (5 shorter events, 0.1 us)
Async XLA Ops:
  4.4 0.8 copy-start
  97.7 1.5 %copy-start.1 = (bf16[256,2048]{1,0:T(8,128)(2,1)S(1)}, bf16[256,2048]{1,0:T(8,128)(2,1)}, u32[]{:S(2)}) copy-start(bf16[256,2048]{1,0:T(8,128)(2,1)} %param.6) | copy-start | bytes 3145732
where the time goes:
time: 130 us; the launch traced here: 129 us
  Pallas kernels  92.4 us (71%)
  matrix products  24.4 us (19%)
  other arithmetic  6.53 us (5%)
  local copies, waits for them, and re-layouts  5.67 us (4%)
    pallas_call x1, Pallas kernels, gather_rows(): pl.pallas_call(functools.partial(gather_kernel, fsdp, rep), out_shape=jax...  92.4 us
    dot_general x1, matrix products, body(): queries = jnp.dot(normed, query_piece, preferred_element_type=jnp.float32)  7.03 us
    dot_general x1, matrix products, body(): lax.dot_general(context, out_piece, (((1,), (1,)), ((), ())), preferred_e...  6.81 us
    unnamed x9, local copies, waits for them, and re-layouts  4.8 us
    sub x1, other arithmetic, body(): expo = jnp.exp(scores - top)  4.57 us
    dot_general x1, matrix products, body(): jnp.einsum('kgqs,skd->qkgd', probs, values_bf, preferred_element_type=jnp...  4.26 us
    dot_general x1, matrix products, body(): keys_raw = jnp.dot(normed, key_piece, preferred_element_type=jnp.float32)  2.61 us

commit v1 on v0

v1 whole, which is shorter than its diff:
```python
import functools

import jax
import jax.numpy as jnp
import numpy as np
from jax import lax
from jax.experimental import pallas as pl
from jax.experimental.pallas import tpu as pltpu
from jax.sharding import PartitionSpec as P

HD = 64
LANES = 128
GROUPS = 2
Z_LINE = 4

rope_base = 500000.0
norm_eps = 1e-05

MESH = pl.DeviceIdType.MESH
NT = (((1,), (1,)), ((), ()))


def rope_tables(tokens, head_dim):
    position = jnp.arange(tokens, dtype=jnp.float32)
    freq = rope_base ** (-(jnp.arange(head_dim // 2, dtype=jnp.float32) * 2.0) / head_dim)
    angle = position[:, None] * freq[None, :]
    cos_table = jnp.concatenate([jnp.cos(angle), jnp.cos(angle)], axis=-1)
    sin_table = jnp.concatenate([jnp.sin(angle), jnp.sin(angle)], axis=-1)
    return (cos_table, sin_table)


def rotate(tensor, cos_table, sin_table):
    half = tensor.shape[-1] // 2
    turned = jnp.concatenate([-tensor[..., half:], tensor[..., :half]], axis=-1)
    return tensor * cos_table + turned * sin_table


def lane_tables(tokens):
    lane = np.arange(LANES)
    freq = np.float64(rope_base) ** (-(lane % (HD // 2)) * 2.0 / HD)
    angle = np.arange(tokens)[:, None] * freq[None, :]
    sign = np.where(lane % HD < HD // 2, -1.0, 1.0)
    return np.cos(angle).astype(np.float32), (np.sin(angle) * sign).astype(np.float32)


def nearest(p, step):
    middle = jnp.where((p == 1) | (p == 2), 1, 0)
    high = step // 2
    low = step % 2
    low = low + middle * high * (1 - 2 * low)
    first = (1 - 2 * (p % 2)) * low
    return p + first + (2 - 4 * (p // 2)) * high


def block_kernel(
    hid_hbm, gain_hbm, wq_hbm, wk_hbm, wv_hbm, wo_hbm, cos_hbm, sin_hbm, out_hbm,
    wa, wv, wo, hid, nrm, acc, ctx, cos_ref, sin_ref, psend, precv, own, outv,
    origin_sem, send_sem, recv_sem, sib_sem, xsend_sem, xrecv_sem, local_sem,
    psend_sem, precv_sem, out_sem,
):
    f, r = lax.axis_index("fsdp"), lax.axis_index("rep")
    z, y = f // 2, f % 2
    x, c = r // 2, r % 2
    tokens, width = hid.shape[1], hid.shape[2]
    rows = wa.shape[4]
    qw = wq_hbm.shape[1] // 2 // GROUPS
    kw = wk_hbm.shape[1] // 2 // GROUPS
    half_out = wo.shape[4]
    cut = half_out - LANES
    span = width // Z_LINE
    partner = (f, (1 - x) * 2 + c)
    sibling = (f, x * 2 + 1 - c)
    across = (z * 2 + 1 - y, r)
    up = (f + 2, r)
    down = (f - 2, r)
    has_up = z + 1 < Z_LINE
    has_down = z >= 1

    def view(kind, g, fs, which):
        if kind == "a":
            return wa.at[g, fs, :, which]
        if kind == "b":
            return wv.at[g, fs, :, which]
        if kind == "oa":
            return wo.at[fs, :, which, :, pl.ds(0, cut)]
        return wo.at[fs, :, which, :, pl.ds(cut, LANES)]

    def index(kind, g):
        return {"a": g, "b": GROUPS + g, "oa": 2 * GROUPS, "ob": 2 * GROUPS + 1}[kind]

    targets = {"up": (0, up, has_up), "down": (1, down, has_down), "across": (2, across, None),
               "sibling": (3, sibling, None)}

    def remote(kind, g, fs, way):
        number, target, _ = targets[way]
        k = index(kind, g)
        ref = view(kind, g, fs, c)
        arrive = sib_sem if way == "sibling" else recv_sem
        return pltpu.make_async_remote_copy(
            src_ref=ref, dst_ref=ref, send_sem=send_sem.at[k, fs, number],
            recv_sem=arrive.at[k, fs], device_id=target, device_id_type=MESH)

    def origin(kind, g, xs, way):
        number, target, _ = targets[way]
        k = index(kind, g)
        ref = view(kind, g, f, c).at[xs]
        arrive = sib_sem if way == "sibling" else recv_sem
        return pltpu.make_async_remote_copy(
            src_ref=ref, dst_ref=ref, send_sem=origin_sem.at[k, xs, number],
            recv_sem=arrive.at[k, f], device_id=target, device_id_type=MESH)

    def when(cond, act):
        if cond is None:
            act()
        else:
            pl.when(cond)(act)

    def spread_origin(kinds, g, xs, act):
        for kind in kinds:
            for way in ("up", "down", "across", "sibling"):
                when(targets[way][2], lambda kind=kind, way=way: act(origin(kind, g, xs, way)))

    def away(kind, g, fs, zs, act):
        when((zs <= z) & has_up, lambda: act(remote(kind, g, fs, "up")))
        when((zs >= z) & has_down, lambda: act(remote(kind, g, fs, "down")))

    def start(copy):
        copy.start()

    def finish(copy):
        copy.wait_send()

    def arrived(kind, g, fs):
        remote(kind, g, fs, "across").wait_recv()

    def near_step(main, side, g, s):
        zs = nearest(z, s)

        @pl.when(s > 0)
        def _():
            fs = zs * 2 + y
            arrived(main, g, fs)
            away(main, g, fs, zs, start)
            remote(main, g, fs, "across").start()
            remote(main, g, fs, "sibling").start()
            arrived(side, g, fs)
            away(side, g, fs, zs, start)
            remote(side, g, fs, "sibling").start()

        fo = zs * 2 + 1 - y
        arrived(side, g, fo)
        away(side, g, fo, zs, start)
        remote(side, g, fo, "sibling").start()

    def far_step(main, g, s):
        fo = nearest(z, s) * 2 + 1 - y
        arrived(main, g, fo)
        remote(main, g, fo, "sibling").start()

    def near_done(main, side, g, s):
        zs = nearest(z, s)

        @pl.when(s > 0)
        def _():
            fs = zs * 2 + y
            away(main, g, fs, zs, finish)
            remote(main, g, fs, "across").wait_send()
            remote(main, g, fs, "sibling").wait_send()
            away(side, g, fs, zs, finish)
            remote(side, g, fs, "sibling").wait_send()

        fo = zs * 2 + 1 - y
        away(side, g, fo, zs, finish)
        remote(side, g, fo, "sibling").wait_send()
        remote(main, g, fo, "sibling").wait_send()

    def sibling_arrived(kinds, g, s):
        zs = nearest(z, s)
        for kind in kinds:
            for col in range(2):
                fs = zs * 2 + col
                ref = view(kind, g, fs, 1 - c)
                pltpu.make_async_remote_copy(
                    src_ref=ref, dst_ref=ref, send_sem=send_sem.at[index(kind, g), fs, 3],
                    recv_sem=sib_sem.at[index(kind, g), fs], device_id=sibling,
                    device_id_type=MESH).wait_recv()

    def q_cols(h, g):
        return pl.ds(pl.multiple_of((h * GROUPS + g) * qw, LANES), qw)

    def k_cols(h, g):
        return pl.ds(pl.multiple_of((h * GROUPS + g) * kw, LANES), kw)

    def o_cols(h):
        return pl.ds(pl.multiple_of(h * half_out, LANES), half_out)

    def local(src, dst, sem):
        return pltpu.make_async_copy(src, dst, local_sem.at[sem])

    for g in range(GROUPS):
        local(wq_hbm.at[:, q_cols(x, g)], wa.at[g, f, x, c, :, pl.ds(0, qw)], 2 * g).start()
        local(wk_hbm.at[:, k_cols(x, g)], wa.at[g, f, x, c, :, pl.ds(qw, kw)], 2 * g).start()
        local(wv_hbm.at[:, k_cols(x, g)], wv.at[g, f, x, c, pl.ds(0, rows)], 2 * g + 1).start()
        local(gain_hbm, wv.at[g, f, x, c, pl.ds(rows, 16)], 2 * g + 1).start()
    local(wo_hbm.at[:, o_cols(x)], wo.at[f, x, c], 4).start()
    local(hid_hbm, hid.at[0], 5).start()
    local(cos_hbm, cos_ref, 6).start()
    local(sin_hbm, sin_ref, 7).start()

    barrier = pltpu.get_barrier_semaphore()
    for target, cond in ((across, None), (up, has_up), (down, has_down), (partner, None),
                         (sibling, None)):
        when(cond, lambda target=target: pl.semaphore_signal(
            barrier, inc=1, device_id=target, device_id_type=MESH))
    pl.semaphore_wait(barrier, 3 + jnp.where(has_up, 1, 0) + jnp.where(has_down, 1, 0))

    def swap(src, dst, number, sem):
        return pltpu.make_async_remote_copy(
            src_ref=src, dst_ref=dst, send_sem=xsend_sem.at[number], recv_sem=xrecv_sem.at[sem],
            device_id=partner, device_id_type=MESH)

    swaps = []
    for g in range(GROUPS):
        h = 1 - x
        swaps += [
            swap(wq_hbm.at[:, q_cols(h, g)], wa.at[g, f, x, c, :, pl.ds(0, qw)], 4 * g, 2 * g),
            swap(wk_hbm.at[:, k_cols(h, g)], wa.at[g, f, x, c, :, pl.ds(qw, kw)], 4 * g + 1, 2 * g),
            swap(wv_hbm.at[:, k_cols(h, g)], wv.at[g, f, x, c, pl.ds(0, rows)], 4 * g + 2, 2 * g + 1),
            swap(gain_hbm, wv.at[g, f, x, c, pl.ds(rows, 16)], 4 * g + 3, 2 * g + 1),
        ]
    swaps.append(swap(hid_hbm, hid.at[1], 8, 4))
    swaps.append(swap(wo_hbm.at[:, o_cols(1 - x)], wo.at[f, x, c], 9, 5))
    for copy in swaps:
        copy.start()

    def swapped(ref, sem):
        swap(ref, ref, 0, sem).wait_recv()

    for g in range(GROUPS):
        local(wa.at[g, f, x, c], wa.at[g, f, x, c], 2 * g).wait()
        local(wv.at[g, f, x, c], wv.at[g, f, x, c], 2 * g + 1).wait()
        spread_origin(("a", "b"), g, x, start)

    def inverse_rms(t):
        value = hid[t].astype(jnp.float32)
        return lax.rsqrt(jnp.mean(value * value, axis=-1, keepdims=True) + norm_eps)

    def gain_row(zs):
        lane = lax.broadcasted_iota(jnp.int32, (1, LANES), 1)
        parts = []
        for col in range(2):
            for xs in range(2):
                low = wv[0, zs * 2 + col, xs, 0, rows:rows + 16, :].astype(jnp.float32)[0:1]
                high = wv[0, zs * 2 + col, xs, 1, rows:rows + 16, :].astype(jnp.float32)[0:1]
                parts.append(jnp.where(lane < rows, low, high))
        return jnp.concatenate(parts, axis=1)

    def normalize(t, zs, inv):
        cols = pl.ds(pl.multiple_of(zs * span, LANES), span)
        value = hid[t, :, cols].astype(jnp.float32) * inv * gain_row(zs)
        nrm[pl.ds(t * tokens, tokens), cols] = value.astype(jnp.bfloat16)

    def project(t, g, zs):
        cols = pl.ds(pl.multiple_of(zs * span, LANES), span)
        left = nrm[pl.ds(t * tokens, tokens), cols]
        fs = pl.ds(zs * 2, 2)
        weight = jnp.concatenate(
            [wa[g, fs].reshape(span, qw + kw), wv[g, fs, :, :, 0:rows, :].reshape(span, kw)], axis=1)
        acc[g, pl.ds(t * tokens, tokens), :] += jnp.dot(
            left, weight, preferred_element_type=jnp.float32)

    acc[...] = jnp.zeros_like(acc)
    local(hid_hbm, hid.at[0], 5).wait()
    inv_own = inverse_rms(0)

    for g in range(GROUPS):
        swapped(wa.at[g, f, 1 - x, c], 2 * g)
        swapped(wv.at[g, f, 1 - x, c], 2 * g + 1)
        spread_origin(("a", "b"), g, 1 - x, start)

    steps = GROUPS * Z_LINE

    def own_chunk(n):
        g, s = n // Z_LINE, n % Z_LINE
        zs = nearest(z, s)
        sibling_arrived(("a", "b"), g, s)

        @pl.when(g == 0)
        def _():
            normalize(0, zs, inv_own)

        project(0, g, zs)

    def qkv_step(n, carry):
        near_step("a", "b", n // Z_LINE, n % Z_LINE)

        @pl.when(n >= 1)
        def _():
            far_step("a", (n - 1) // Z_LINE, (n - 1) % Z_LINE)

        @pl.when(n >= 2)
        def _():
            own_chunk(n - 2)

        return carry

    lax.fori_loop(0, steps - 1, qkv_step, 0)

    swap(hid_hbm, hid.at[1], 8, 4).wait_recv()
    inv_other = inverse_rms(1)

    def other_first(zs, carry):
        normalize(1, zs, inv_other)
        project(1, 0, zs)
        return carry

    lax.fori_loop(0, Z_LINE, other_first, 0)
    near_step("a", "b", GROUPS - 1, Z_LINE - 1)
    far_step("a", GROUPS - 1, Z_LINE - 2)

    local(wo_hbm.at[:, o_cols(x)], wo.at[f, x, c], 4).wait()
    spread_origin(("oa", "ob"), 0, x, start)
    swapped(wo.at[f, 1 - x, c], 5)
    spread_origin(("oa", "ob"), 0, 1 - x, start)
    own_chunk(steps - 3)

    local(cos_hbm, cos_ref, 6).wait()
    local(sin_hbm, sin_ref, 7).wait()

    def attend(g, t):
        base = pl.multiple_of(t * tokens, tokens)
        span_rows = pl.ds(base, tokens)
        lane = lax.broadcasted_iota(jnp.int32, (tokens, LANES), 1)
        first = lane % HD < HD // 2
        left_head = lane < HD

        def turn(tile):
            turned = jnp.where(first, pltpu.roll(tile, LANES - HD // 2, 1),
                               pltpu.roll(tile, HD // 2, 1))
            return tile * cos_ref[...] + turned * sin_ref[...]

        key = turn(acc[g, span_rows, qw:qw + kw])
        value = acc[g, span_rows, qw + kw:qw + 2 * kw]
        key_other, value_other = pltpu.roll(key, HD, 1), pltpu.roll(value, HD, 1)
        for j in range(kw // HD):
            def low_high(tile, tile_other):
                low = tile if j == 0 else tile_other
                high = tile_other if j == 0 else tile
                zero = jnp.zeros_like(tile)
                return (jnp.where(left_head, low, zero).astype(jnp.bfloat16),
                        jnp.where(left_head, zero, high).astype(jnp.bfloat16))

            key_low, key_high = low_high(key, key_other)
            value_low, value_high = low_high(value, value_other)
            heads = qw // (kw // HD)
            query = []
            for p in range(heads // LANES):
                at = j * heads + p * LANES
                tile = turn(acc[g, span_rows, at:at + LANES])
                query.append(tile.astype(jnp.bfloat16) * jnp.bfloat16(HD ** -0.5))
            block = tokens // 2
            for b in range(2):
                seen = (b + 1) * block
                rows_q = slice(b * block, (b + 1) * block)
                stacked = jnp.concatenate([q[rows_q] for q in query], axis=0)
                keys = jnp.concatenate([key_low[:seen], key_high[:seen]], axis=0)
                values = jnp.concatenate([value_low[:seen], value_high[:seen]], axis=0)
                scores = lax.dot_general(stacked, keys, NT, preferred_element_type=jnp.float32)
                count = stacked.shape[0]
                at_row = lax.broadcasted_iota(jnp.int32, (count, seen), 0) % block + b * block
                at_col = lax.broadcasted_iota(jnp.int32, (count, seen), 1)
                open_ = at_row >= at_col
                probs = []
                for e in range(2):
                    part = jnp.where(open_, scores[:, e * seen:(e + 1) * seen], -1e30)
                    top = jnp.max(part, axis=-1, keepdims=True)
                    expo = jnp.exp(part - top)
                    total = jnp.sum(expo, axis=-1, keepdims=True)
                    probs.append((expo * (1.0 / total)).astype(jnp.bfloat16))
                mixed = jnp.dot(jnp.concatenate(probs, axis=1), values,
                                preferred_element_type=jnp.float32).astype(jnp.bfloat16)
                for p in range(heads // LANES):
                    at = g * qw + j * heads + p * LANES
                    ctx[pl.ds(base + b * block, block), at:at + LANES] = (
                        mixed[p * block:(p + 1) * block])

    def attend_first(t, carry):
        attend(0, t)
        return carry

    lax.fori_loop(0, 2, attend_first, 0)

    far_step("a", GROUPS - 1, Z_LINE - 1)
    own_chunk(steps - 2)
    near_step("oa", "ob", 0, 0)
    own_chunk(steps - 1)

    def other_second(zs, carry):
        project(1, 1, zs)
        return carry

    lax.fori_loop(0, Z_LINE, other_second, 0)
    attend(1, 1)

    def out_weight(s):
        return wo[pl.ds(nearest(z, s) * 2, 2)].reshape(span, half_out)

    def share(s):
        return pltpu.make_async_remote_copy(
            src_ref=psend.at[s], dst_ref=precv.at[s], send_sem=psend_sem.at[s],
            recv_sem=precv_sem.at[s], device_id=partner, device_id_type=MESH)

    def out_other(s):
        part = lax.dot_general(ctx[tokens:2 * tokens, :], out_weight(s), NT,
                               preferred_element_type=jnp.float32)
        psend[s] = part.astype(jnp.bfloat16)
        share(s).start()

    def out_own(s):
        cols = pl.ds(pl.multiple_of(nearest(z, s) * span, LANES), span)
        part = lax.dot_general(ctx[0:tokens, :], out_weight(s), NT,
                               preferred_element_type=jnp.float32)
        own[s] = hid[0, :, cols].astype(jnp.float32) + part

    def emit(s):
        cols = pl.ds(pl.multiple_of(nearest(z, s) * span, LANES), span)
        return pltpu.make_async_copy(outv.at[s], out_hbm.at[:, cols], out_sem.at[s])

    def close(s):
        share(s).wait_recv()
        outv[s] = (own[s] + precv[s].astype(jnp.float32)).astype(jnp.bfloat16)
        emit(s).start()

    far_step("oa", 0, 0)
    sibling_arrived(("oa", "ob"), 0, 0)
    out_other(0)
    near_step("oa", "ob", 0, 1)
    attend(1, 0)
    out_own(0)

    def out_step(s, carry):
        far_step("oa", 0, s)

        @pl.when(s < Z_LINE - 1)
        def _():
            near_step("oa", "ob", 0, s + 1)

        sibling_arrived(("oa", "ob"), 0, s)
        out_other(s)
        out_own(s)
        return carry

    lax.fori_loop(1, Z_LINE, out_step, 0)

    def close_step(s, carry):
        close(s)
        return carry

    lax.fori_loop(0, Z_LINE, close_step, 0)

    for copy in swaps:
        copy.wait_send()
    for g in range(GROUPS):
        for xs in range(2):
            spread_origin(("a", "b"), g, xs, finish)
    for xs in range(2):
        spread_origin(("oa", "ob"), 0, xs, finish)

    def drain_qkv(n, carry):
        near_done("a", "b", n // Z_LINE, n % Z_LINE)
        return carry

    lax.fori_loop(0, steps, drain_qkv, 0)

    def drain_out(s, carry):
        near_done("oa", "ob", 0, s)
        share(s).wait_send()
        emit(s).wait()
        return carry

    lax.fori_loop(0, Z_LINE, drain_out, 0)


def fused(hidden, attn_gain, w_query, w_key, w_value, w_out):
    tokens, width = hidden.shape
    rows, width_query = w_query.shape
    width_kv = w_key.shape[1]
    fsdp = Z_LINE * 2
    qw, kw = width_query // 2 // GROUPS, width_kv // 2 // GROUPS
    half_out = width_query // 2
    span = width // Z_LINE
    gain = jnp.broadcast_to(jnp.concatenate([attn_gain, attn_gain])[None, :], (16, LANES))
    cos_table, sin_table = lane_tables(tokens)
    kinds = 2 * GROUPS + 2
    dma = pltpu.SemaphoreType.DMA
    return pl.pallas_call(
        block_kernel,
        out_shape=jax.ShapeDtypeStruct((tokens, width), hidden.dtype),
        in_specs=[pl.BlockSpec(memory_space=pl.ANY)] * 8,
        out_specs=pl.BlockSpec(memory_space=pl.ANY),
        scratch_shapes=[
            pltpu.VMEM((GROUPS, fsdp, 2, 2, rows, qw + kw), jnp.bfloat16),
            pltpu.VMEM((GROUPS, fsdp, 2, 2, rows + 16, kw), jnp.bfloat16),
            pltpu.VMEM((fsdp, 2, 2, rows, half_out), jnp.bfloat16),
            pltpu.VMEM((2, tokens, width), jnp.bfloat16),
            pltpu.VMEM((2 * tokens, width), jnp.bfloat16),
            pltpu.VMEM((GROUPS, 2 * tokens, qw + 2 * kw), jnp.float32),
            pltpu.VMEM((2 * tokens, half_out), jnp.bfloat16),
            pltpu.VMEM((tokens, LANES), jnp.float32),
            pltpu.VMEM((tokens, LANES), jnp.float32),
            pltpu.VMEM((Z_LINE, tokens, span), jnp.bfloat16),
            pltpu.VMEM((Z_LINE, tokens, span), jnp.bfloat16),
            pltpu.VMEM((Z_LINE, tokens, span), jnp.float32),
            pltpu.VMEM((Z_LINE, tokens, span), jnp.bfloat16),
            dma((kinds, 2, 4)),
            dma((kinds, fsdp, 4)),
            dma((kinds, fsdp)),
            dma((kinds, fsdp)),
            dma((10,)),
            dma((6,)),
            dma((8,)),
            dma((Z_LINE,)),
            dma((Z_LINE,)),
            dma((Z_LINE,)),
        ],
        compiler_params=pltpu.CompilerParams(
            collective_id=0, has_side_effects=True, vmem_limit_bytes=60 * 1024 * 1024),
        name="attention_block",
    )(hidden, gain, w_query, w_key, w_value, w_out.T, jnp.asarray(cos_table), jnp.asarray(sin_table))


def fits(fsdp, rep, hidden, w_query, w_key, w_out):
    tokens, width = hidden.shape
    rows, width_query = w_query.shape
    return (
        rep == 4
        and fsdp == 2 * Z_LINE
        and 2 * rows == LANES
        and width == fsdp * rep * rows
        and w_out.shape == (width_query, rows)
        and w_key.shape[1] == 2 * GROUPS * LANES
        and width_query == 4 * w_key.shape[1]
        and tokens % LANES == 0
    )


def body(fsdp, rep, hidden, attn_gain, w_query, w_key, w_value, w_out):
    if fits(fsdp, rep, hidden, w_query, w_key, w_out):
        return fused(hidden, attn_gain, w_query, w_key, w_value, w_out)
    tokens = hidden.shape[0]
    head_dim = HD
    width_query = w_query.shape[1]
    width_kv = w_key.shape[1]
    kv_count = width_kv // head_dim
    group = width_query // width_kv
    x_float = hidden.astype(jnp.float32)
    inv_rms = lax.rsqrt(jnp.mean(x_float * x_float, axis=-1, keepdims=True) + norm_eps)
    width_rows = w_query.shape[0]
    packed = jnp.concatenate(
        [w_query, w_key, w_value, w_out.T, jnp.broadcast_to(attn_gain[:, None], (width_rows, 128))],
        axis=1,
    )
    packed = lax.all_gather(packed, ("fsdp", "rep"), axis=0, tiled=True)
    cut_key = width_query
    cut_value = cut_key + width_kv
    cut_out = cut_value + width_kv
    cut_gain = cut_out + w_out.shape[0]
    query_piece = packed[:, :cut_key]
    key_piece = packed[:, cut_key:cut_value]
    value_piece = packed[:, cut_value:cut_out]
    out_piece = packed[:, cut_out:cut_gain]
    gain_piece = packed[:, cut_gain]
    normed = (x_float * inv_rms * gain_piece.astype(jnp.float32)[None, :]).astype(jnp.bfloat16)
    queries = jnp.dot(normed, query_piece, preferred_element_type=jnp.float32)
    keys_raw = jnp.dot(normed, key_piece, preferred_element_type=jnp.float32)
    values_raw = jnp.dot(normed, value_piece, preferred_element_type=jnp.float32)
    cos_table, sin_table = rope_tables(tokens, head_dim)
    queries = queries.reshape(tokens, kv_count, group, head_dim)
    keys_raw = keys_raw.reshape(tokens, kv_count, head_dim)
    values_bf = values_raw.reshape(tokens, kv_count, head_dim).astype(jnp.bfloat16)
    rope_queries = rotate(queries, cos_table[:, None, None, :], sin_table[:, None, None, :]).astype(
        jnp.bfloat16
    )
    rope_keys = rotate(keys_raw, cos_table[:, None, :], sin_table[:, None, :]).astype(jnp.bfloat16)
    scores = jnp.einsum(
        "qkgd,skd->kgqs", rope_queries, rope_keys, preferred_element_type=jnp.float32
    ) * head_dim ** (-0.5)
    causal = jnp.arange(tokens)[:, None] >= jnp.arange(tokens)[None, :]
    scores = jnp.where(causal[None, None, :, :], scores, -1e30)
    top = jnp.max(scores, axis=-1, keepdims=True)
    expo = jnp.exp(scores - top)
    probs = (expo / jnp.sum(expo, axis=-1, keepdims=True)).astype(jnp.bfloat16)
    context = jnp.einsum("kgqs,skd->qkgd", probs, values_bf, preferred_element_type=jnp.float32)
    context = context.reshape(tokens, width_query).astype(jnp.bfloat16)
    branch = lax.dot_general(
        context, out_piece, (((1,), (1,)), ((), ())), preferred_element_type=jnp.float32
    )
    return (x_float + branch).astype(jnp.bfloat16)


def solution(mesh):
    placed = (
        P(("fsdp", "rep"), None),
        P(("fsdp", "rep")),
        P(("fsdp", "rep"), None),
        P(("fsdp", "rep"), None),
        P(("fsdp", "rep"), None),
        P(None, ("fsdp", "rep")),
    )
    return jax.shard_map(
        functools.partial(body, mesh.shape["fsdp"], mesh.shape["rep"]),
        mesh=mesh,
        in_specs=placed,
        out_specs=P(("fsdp", "rep"), None),
        check_vma=False,
    )
```

time: 130 us -> 94.2 us (0.72)
  matrix products: 24.4 us -> 0 us
  other arithmetic: 6.53 us -> 0.08 us
  local copies, waits for them, and re-layouts: 5.67 us -> 3.56 us
  Pallas kernels: 92.4 us -> 90.4 us
    dot_general x6 -> x0, matrix products: 24.4 us -> none  [the longest x1 7.03 us: body(): queries = jnp.dot(normed, query_piece, preferred_element_type=jnp.float32)]
    sub x1 -> x0, other arithmetic: 4.57 us -> none  [body(): expo = jnp.exp(scores - top)]
    pallas_call x1, Pallas kernels: 92.4 us -> 90.4 us  [fused(): pl.pallas_call(block_kernel, out_shape=jax.ShapeDtypeStruct((tokens, widt...]
    unnamed x9 -> x3, local copies, waits for them, and re-layouts: 4.8 us -> 2.96 us
where the time goes in v1:
time: 94.2 us; the launch traced here: 94.1 us
  Pallas kernels  90.4 us (96%)
  local copies, waits for them, and re-layouts  3.56 us (4%)
    pallas_call x1, Pallas kernels, fused(): pl.pallas_call(block_kernel, out_shape=jax.ShapeDtypeStruct((tokens, widt...  90.4 us
    unnamed x3, local copies, waits for them, and re-layouts  2.96 us

profile of v1, /device:TPU:0, one launch (start us, length us, event | category | flops | bytes accessed | tf_op | source)
XLA Modules:
  0.0 94.1 jit_solution(7014866959526155635)
XLA Ops:
  0.0 0.0 copy-start
  0.0 0.7 copy-done
  0.7 0.1 pad_maximum_fusion
  0.7 0.6 broadcast_in_dim.2.gain_hbm
  1.3 90.4 %attention_block.1 = bf16[256,2048]{1,0:T(8,128)(2,1)} custom-call(bf16[256,2048]{1,0:T(8,128)(2,1)} %hid_hbm.1, bf16[16,128]{1,0:T(8,128)(2,1)} %broadcast_in_dim.2.gain_hbm, bf16[64,2048]{1,0:T(8,128)(2,1)} %wq_hbm.1, bf16[64,512]{1,0:T(8,128)(2,1)} %wk_hbm.1, bf16[64,512]{1,0:T(8,128)(2,1)} %wv_hbm.1, bf16[64,2048]{1,0:T(8,128)(2,1)} %bitcast.1, ...), custom_call_target="tpu_custom_call" | custom-call | tf_op jit(solution)/shard_map/attention_block/pallas_call | solution.py:496
  91.7 2.3 %copy.10 = bf16[256,2048]{1,0:T(8,128)(2,1)} copy(bf16[256,2048]{1,0:T(8,128)(2,1)} %attention_block.1) | data formatting | bytes 2097152
Async XLA Ops:
  0.0 0.7 copy-start

commit v2 on v1

--- a/solution.py
+++ b/solution.py
@@ -19,6 +19,80 @@
 MESH = pl.DeviceIdType.MESH
 NT = (((1,), (1,)), ((), ()))
 
+PIECES = (("a", 0), ("a", 1), ("b", 0), ("b", 1), ("oa", 0), ("ob", 0))
+EDGE_PLAN = (
+    (100, 102, 101, 103, 1, 20, 9, 17, 28, 2, 4, 5, 13, 3, 22,),
+    (21, 26, 18, 12, 6,),
+    (25, 104, 7, 19,),
+    (23,),
+    (10,),
+    (),
+    (),
+    (11, 29,),
+    (27, 105, 14,),
+    (),
+    (),
+    (30, 15,),
+    (31,),
+    (),
+    (36,),
+    (44, 33,),
+    (),
+    (34, 41,),
+    (45, 37,),
+    (),
+    (),
+    (),
+    (),
+    (35, 38, 46,),
+    (42,),
+    (47,),
+    (43, 39,),
+    (),
+    (),
+    (),
+    (),
+    (),
+    (),
+    (),
+)
+MIDDLE_PLAN = (
+    (100, 102, 101, 103, 0, 21, 16, 5, 18, 2, 20, 3, 24, 23,),
+    (13, 6, 22, 26, 19, 4, 8, 10,),
+    (),
+    (28, 7,),
+    (11,),
+    (27, 12, 29, 14,),
+    (104,),
+    (),
+    (),
+    (30, 31, 105,),
+    (),
+    (15,),
+    (),
+    (32, 34,),
+    (37, 45,),
+    (),
+    (40,),
+    (44,),
+    (),
+    (35,),
+    (46, 36,),
+    (42,),
+    (),
+    (47, 43, 38,),
+    (),
+    (),
+    (39,),
+    (),
+    (),
+    (),
+    (),
+    (),
+    (),
+    (),
+)
+
 
 def rope_tables(tokens, head_dim):
     position = jnp.arange(tokens, dtype=jnp.float32)
@@ -53,10 +127,10 @@
 
 
 def block_kernel(
-    hid_hbm, gain_hbm, wq_hbm, wk_hbm, wv_hbm, wo_hbm, cos_hbm, sin_hbm, out_hbm,
-    wa, wv, wo, hid, nrm, acc, ctx, cos_ref, sin_ref, psend, precv, own, outv,
+    hid_hbm, gain_hbm, wq_hbm, wk_hbm, wv_hbm, wo_hbm, cos_hbm, sin_hbm, out_ref,
+    wa, wv, woa, wob, hid, nrm, acc, ctx, cos_ref, sin_ref, psend, precv, own, gain_in, gain_tile,
     origin_sem, send_sem, recv_sem, sib_sem, xsend_sem, xrecv_sem, local_sem,
-    psend_sem, precv_sem, out_sem,
+    psend_sem, precv_sem,
 ):
     f, r = lax.axis_index("fsdp"), lax.axis_index("rep")
     z, y = f // 2, f % 2
@@ -65,16 +139,22 @@
     rows = wa.shape[4]
     qw = wq_hbm.shape[1] // 2 // GROUPS
     kw = wk_hbm.shape[1] // 2 // GROUPS
-    half_out = wo.shape[4]
-    cut = half_out - LANES
+    cut = woa.shape[4]
+    half_out = cut + wob.shape[4]
     span = width // Z_LINE
     partner = (f, (1 - x) * 2 + c)
     sibling = (f, x * 2 + 1 - c)
     across = (z * 2 + 1 - y, r)
-    up = (f + 2, r)
-    down = (f - 2, r)
-    has_up = z + 1 < Z_LINE
-    has_down = z >= 1
+    low_half = z < Z_LINE // 2
+    edge = (z == 0) | (z == Z_LINE - 1)
+    middle = jnp.logical_not(edge)
+    toward = jnp.where(low_half, 2, -2)
+    outward = (f - toward, r)
+    inward = (f + toward, r)
+    mine = jnp.where(edge, 0, 1)
+
+    def at_line(k):
+        return jnp.where(low_half, k, Z_LINE - 1 - k)
 
     def view(kind, g, fs, which):
         if kind == "a":
@@ -82,17 +162,17 @@
         if kind == "b":
             return wv.at[g, fs, :, which]
         if kind == "oa":
-            return wo.at[fs, :, which, :, pl.ds(0, cut)]
-        return wo.at[fs, :, which, :, pl.ds(cut, LANES)]
+            return woa.at[fs, :, which]
+        return wob.at[fs, :, which]
 
     def index(kind, g):
         return {"a": g, "b": GROUPS + g, "oa": 2 * GROUPS, "ob": 2 * GROUPS + 1}[kind]
 
-    targets = {"up": (0, up, has_up), "down": (1, down, has_down), "across": (2, across, None),
-               "sibling": (3, sibling, None)}
+    targets = {"outward": (0, outward), "inward": (1, inward), "across": (2, across),
+               "sibling": (3, sibling)}
 
     def remote(kind, g, fs, way):
-        number, target, _ = targets[way]
+        number, target = targets[way]
         k = index(kind, g)
         ref = view(kind, g, fs, c)
         arrive = sib_sem if way == "sibling" else recv_sem
@@ -101,7 +181,7 @@
             recv_sem=arrive.at[k, fs], device_id=target, device_id_type=MESH)
 
     def origin(kind, g, xs, way):
-        number, target, _ = targets[way]
+        number, target = targets[way]
         k = index(kind, g)
         ref = view(kind, g, f, c).at[xs]
         arrive = sib_sem if way == "sibling" else recv_sem
@@ -109,70 +189,53 @@
             src_ref=ref, dst_ref=ref, send_sem=origin_sem.at[k, xs, number],
             recv_sem=arrive.at[k, f], device_id=target, device_id_type=MESH)
 
-    def when(cond, act):
-        if cond is None:
-            act()
-        else:
-            pl.when(cond)(act)
-
-    def spread_origin(kinds, g, xs, act):
+    def relay(piece, own):
+        kind, g = PIECES[piece // 8]
+        col, k = piece // 4 % 2, piece % 4
+        main = kind in ("a", "oa")
+        fs = at_line(k) * 2 + (y if col == 0 else 1 - y)
+        remote(kind, g, fs, "across").wait_recv()
+        if not (main and col == 1):
+            if k >= own and own > 0:
+                remote(kind, g, fs, "outward").start()
+            if k <= own:
+                remote(kind, g, fs, "inward").start()
+            if main and col == 0:
+                remote(kind, g, fs, "across").start()
+        remote(kind, g, fs, "sibling").start()
+
+    def sent(kind, g, k):
+        main = kind in ("a", "oa")
+        out_ok, in_ok = middle & (k >= mine), k <= mine
+
+        def column(col, side):
+            fs = at_line(k) * 2 + (y if col == 0 else 1 - y)
+            if side:
+                pl.when(out_ok)(lambda: remote(kind, g, fs, "outward").wait_send())
+                pl.when(in_ok)(lambda: remote(kind, g, fs, "inward").wait_send())
+            if main and col == 0:
+                remote(kind, g, fs, "across").wait_send()
+            remote(kind, g, fs, "sibling").wait_send()
+
+        pl.when(k != mine)(lambda: column(0, True))
+        column(1, not main)
+
+    def origin_ways(kinds, g, xs, act, middle_chip):
         for kind in kinds:
-            for way in ("up", "down", "across", "sibling"):
-                when(targets[way][2], lambda kind=kind, way=way: act(origin(kind, g, xs, way)))
-
-    def away(kind, g, fs, zs, act):
-        when((zs <= z) & has_up, lambda: act(remote(kind, g, fs, "up")))
-        when((zs >= z) & has_down, lambda: act(remote(kind, g, fs, "down")))
+            for way in targets:
+                if way == "outward":
+                    if middle_chip is True:
+                        act(origin(kind, g, xs, way))
+                    elif middle_chip is not False:
+                        pl.when(middle_chip)(lambda kind=kind: act(origin(kind, g, xs, "outward")))
+                else:
+                    act(origin(kind, g, xs, way))
 
     def start(copy):
         copy.start()
 
     def finish(copy):
         copy.wait_send()
-
-    def arrived(kind, g, fs):
-        remote(kind, g, fs, "across").wait_recv()
-
-    def near_step(main, side, g, s):
-        zs = nearest(z, s)
-
-        @pl.when(s > 0)
-        def _():
-            fs = zs * 2 + y
-            arrived(main, g, fs)
-            away(main, g, fs, zs, start)
-            remote(main, g, fs, "across").start()
-            remote(main, g, fs, "sibling").start()
-            arrived(side, g, fs)
-            away(side, g, fs, zs, start)
-            remote(side, g, fs, "sibling").start()
-
-        fo = zs * 2 + 1 - y
-        arrived(side, g, fo)
-        away(side, g, fo, zs, start)
-        remote(side, g, fo, "sibling").start()
-
-    def far_step(main, g, s):
-        fo = nearest(z, s) * 2 + 1 - y
-        arrived(main, g, fo)
-        remote(main, g, fo, "sibling").start()
-
-    def near_done(main, side, g, s):
-        zs = nearest(z, s)
-
-        @pl.when(s > 0)
-        def _():
-            fs = zs * 2 + y
-            away(main, g, fs, zs, finish)
-            remote(main, g, fs, "across").wait_send()
-            remote(main, g, fs, "sibling").wait_send()
-            away(side, g, fs, zs, finish)
-            remote(side, g, fs, "sibling").wait_send()
-
-        fo = zs * 2 + 1 - y
-        away(side, g, fo, zs, finish)
-        remote(side, g, fo, "sibling").wait_send()
-        remote(main, g, fo, "sibling").wait_send()
 
     def sibling_arrived(kinds, g, s):
         zs = nearest(z, s)
@@ -191,28 +254,45 @@
     def k_cols(h, g):
         return pl.ds(pl.multiple_of((h * GROUPS + g) * kw, LANES), kw)
 
-    def o_cols(h):
-        return pl.ds(pl.multiple_of(h * half_out, LANES), half_out)
+    def oa_cols(h):
+        return pl.ds(pl.multiple_of(h * half_out, LANES), cut)
+
+    def ob_cols(h):
+        return pl.ds(pl.multiple_of(h * half_out + cut, LANES), half_out - cut)
 
     def local(src, dst, sem):
         return pltpu.make_async_copy(src, dst, local_sem.at[sem])
 
+    local(gain_hbm, gain_in, 9).start()
     for g in range(GROUPS):
         local(wq_hbm.at[:, q_cols(x, g)], wa.at[g, f, x, c, :, pl.ds(0, qw)], 2 * g).start()
         local(wk_hbm.at[:, k_cols(x, g)], wa.at[g, f, x, c, :, pl.ds(qw, kw)], 2 * g).start()
         local(wv_hbm.at[:, k_cols(x, g)], wv.at[g, f, x, c, pl.ds(0, rows)], 2 * g + 1).start()
-        local(gain_hbm, wv.at[g, f, x, c, pl.ds(rows, 16)], 2 * g + 1).start()
-    local(wo_hbm.at[:, o_cols(x)], wo.at[f, x, c], 4).start()
-    local(hid_hbm, hid.at[0], 5).start()
-    local(cos_hbm, cos_ref, 6).start()
-    local(sin_hbm, sin_ref, 7).start()
+    local(wo_hbm.at[:, oa_cols(x)], woa.at[f, x, c], 4).start()
+    local(wo_hbm.at[:, ob_cols(x)], wob.at[f, x, c], 5).start()
+    local(hid_hbm, hid.at[0], 6).start()
+    local(cos_hbm, cos_ref, 7).start()
+    local(sin_hbm, sin_ref, 8).start()
+
+    def inverse_rms(t):
+        value = hid[t].astype(jnp.float32)
+        return lax.rsqrt(jnp.mean(value * value, axis=-1, keepdims=True) + norm_eps)
 
     barrier = pltpu.get_barrier_semaphore()
-    for target, cond in ((across, None), (up, has_up), (down, has_down), (partner, None),
-                         (sibling, None)):
-        when(cond, lambda target=target: pl.semaphore_signal(
-            barrier, inc=1, device_id=target, device_id_type=MESH))
-    pl.semaphore_wait(barrier, 3 + jnp.where(has_up, 1, 0) + jnp.where(has_down, 1, 0))
+    for target in (across, inward, partner, sibling):
+        pl.semaphore_signal(barrier, inc=1, device_id=target, device_id_type=MESH)
+    pl.when(middle)(lambda: pl.semaphore_signal(
+        barrier, inc=1, device_id=outward, device_id_type=MESH))
+    acc[...] = jnp.zeros_like(acc)
+    local(gain_hbm, gain_in, 9).wait()
+    gain = gain_in[...].astype(jnp.float32)
+    gain = jnp.broadcast_to(jnp.concatenate([gain, gain], axis=1), (16, LANES))
+    gain_tile[...] = gain.astype(jnp.bfloat16)
+    for g in range(GROUPS):
+        wv[g, f, x, c, rows:rows + 16, :] = gain.astype(jnp.bfloat16)
+    local(hid_hbm, hid.at[0], 6).wait()
+    inv_own = inverse_rms(0)
+    pl.semaphore_wait(barrier, 4 + mine)
 
     def swap(src, dst, number, sem):
         return pltpu.make_async_remote_copy(
@@ -226,24 +306,48 @@
             swap(wq_hbm.at[:, q_cols(h, g)], wa.at[g, f, x, c, :, pl.ds(0, qw)], 4 * g, 2 * g),
             swap(wk_hbm.at[:, k_cols(h, g)], wa.at[g, f, x, c, :, pl.ds(qw, kw)], 4 * g + 1, 2 * g),
             swap(wv_hbm.at[:, k_cols(h, g)], wv.at[g, f, x, c, pl.ds(0, rows)], 4 * g + 2, 2 * g + 1),
-            swap(gain_hbm, wv.at[g, f, x, c, pl.ds(rows, 16)], 4 * g + 3, 2 * g + 1),
+            swap(gain_tile, wv.at[g, f, x, c, pl.ds(rows, 16)], 4 * g + 3, 2 * g + 1),
         ]
-    swaps.append(swap(hid_hbm, hid.at[1], 8, 4))
-    swaps.append(swap(wo_hbm.at[:, o_cols(1 - x)], wo.at[f, x, c], 9, 5))
+    swaps.append(swap(hid_hbm, hid.at[1], 8, 6))
+    swaps.append(swap(wo_hbm.at[:, oa_cols(1 - x)], woa.at[f, x, c], 9, 4))
+    swaps.append(swap(wo_hbm.at[:, ob_cols(1 - x)], wob.at[f, x, c], 10, 5))
     for copy in swaps:
         copy.start()
 
     def swapped(ref, sem):
         swap(ref, ref, 0, sem).wait_recv()
 
-    for g in range(GROUPS):
-        local(wa.at[g, f, x, c], wa.at[g, f, x, c], 2 * g).wait()
-        local(wv.at[g, f, x, c], wv.at[g, f, x, c], 2 * g + 1).wait()
-        spread_origin(("a", "b"), g, x, start)
-
-    def inverse_rms(t):
-        value = hid[t].astype(jnp.float32)
-        return lax.rsqrt(jnp.mean(value * value, axis=-1, keepdims=True) + norm_eps)
+    def ready(stage, xs):
+        part = x if xs == 0 else 1 - x
+        if stage < GROUPS:
+            refs = ((wa.at[stage, f, part, c], 2 * stage),
+                    (wv.at[stage, f, part, c, pl.ds(0, rows + 16 * xs)], 2 * stage + 1))
+        else:
+            refs = ((woa.at[f, part, c], 4), (wob.at[f, part, c], 5))
+        for ref, sem in refs:
+            if xs == 0:
+                local(ref, ref, sem).wait()
+            else:
+                swapped(ref, sem)
+
+    def stretch(number, cond=None):
+        for plan, here, own in ((EDGE_PLAN, edge, 0), (MIDDLE_PLAN, middle, 1)):
+            if plan[number]:
+                def run(plan=plan, own=own):
+                    for code in plan[number]:
+                        if code < 100:
+                            relay(code, own)
+                        else:
+                            stage, xs = (code - 100) // 2, (code - 100) % 2
+                            ready(stage, xs)
+                            kinds = ("a", "b") if stage < GROUPS else ("oa", "ob")
+                            origin_ways(kinds, stage % GROUPS, x if xs == 0 else 1 - x, start,
+                                        own == 1)
+                pl.when(here if cond is None else here & cond)(run)
+
+    def stretches(first, step, count):
+        for number in range(count):
+            stretch(first + number, step == number)
 
     def gain_row(zs):
         lane = lax.broadcasted_iota(jnp.int32, (1, LANES), 1)
@@ -269,66 +373,8 @@
         acc[g, pl.ds(t * tokens, tokens), :] += jnp.dot(
             left, weight, preferred_element_type=jnp.float32)
 
-    acc[...] = jnp.zeros_like(acc)
-    local(hid_hbm, hid.at[0], 5).wait()
-    inv_own = inverse_rms(0)
-
-    for g in range(GROUPS):
-        swapped(wa.at[g, f, 1 - x, c], 2 * g)
-        swapped(wv.at[g, f, 1 - x, c], 2 * g + 1)
-        spread_origin(("a", "b"), g, 1 - x, start)
-
-    steps = GROUPS * Z_LINE
-
-    def own_chunk(n):
-        g, s = n // Z_LINE, n % Z_LINE
-        zs = nearest(z, s)
-        sibling_arrived(("a", "b"), g, s)
-
-        @pl.when(g == 0)
-        def _():
-            normalize(0, zs, inv_own)
-
-        project(0, g, zs)
-
-    def qkv_step(n, carry):
-        near_step("a", "b", n // Z_LINE, n % Z_LINE)
-
-        @pl.when(n >= 1)
-        def _():
-            far_step("a", (n - 1) // Z_LINE, (n - 1) % Z_LINE)
-
-        @pl.when(n >= 2)
-        def _():
-            own_chunk(n - 2)
-
-        return carry
-
-    lax.fori_loop(0, steps - 1, qkv_step, 0)
-
-    swap(hid_hbm, hid.at[1], 8, 4).wait_recv()
-    inv_other = inverse_rms(1)
-
-    def other_first(zs, carry):
-        normalize(1, zs, inv_other)
-        project(1, 0, zs)
-        return carry
-
-    lax.fori_loop(0, Z_LINE, other_first, 0)
-    near_step("a", "b", GROUPS - 1, Z_LINE - 1)
-    far_step("a", GROUPS - 1, Z_LINE - 2)
-
-    local(wo_hbm.at[:, o_cols(x)], wo.at[f, x, c], 4).wait()
-    spread_origin(("oa", "ob"), 0, x, start)
-    swapped(wo.at[f, 1 - x, c], 5)
-    spread_origin(("oa", "ob"), 0, 1 - x, start)
-    own_chunk(steps - 3)
-
-    local(cos_hbm, cos_ref, 6).wait()
-    local(sin_hbm, sin_ref, 7).wait()
-
     def attend(g, t):
-        base = pl.multiple_of(t * tokens, tokens)
+        base = t * tokens
         span_rows = pl.ds(base, tokens)
         lane = lax.broadcasted_iota(jnp.int32, (tokens, LANES), 1)
         first = lane % HD < HD // 2
@@ -384,26 +430,10 @@
                     ctx[pl.ds(base + b * block, block), at:at + LANES] = (
                         mixed[p * block:(p + 1) * block])
 
-    def attend_first(t, carry):
-        attend(0, t)
-        return carry
-
-    lax.fori_loop(0, 2, attend_first, 0)
-
-    far_step("a", GROUPS - 1, Z_LINE - 1)
-    own_chunk(steps - 2)
-    near_step("oa", "ob", 0, 0)
-    own_chunk(steps - 1)
-
-    def other_second(zs, carry):
-        project(1, 1, zs)
-        return carry
-
-    lax.fori_loop(0, Z_LINE, other_second, 0)
-    attend(1, 1)
-
     def out_weight(s):
-        return wo[pl.ds(nearest(z, s) * 2, 2)].reshape(span, half_out)
+        fs = pl.ds(nearest(z, s) * 2, 2)
+        return jnp.concatenate(
+            [woa[fs].reshape(span, cut), wob[fs].reshape(span, half_out - cut)], axis=1)
 
     def share(s):
         return pltpu.make_async_remote_copy(
@@ -422,63 +452,102 @@
                                preferred_element_type=jnp.float32)
         own[s] = hid[0, :, cols].astype(jnp.float32) + part
 
-    def emit(s):
-        cols = pl.ds(pl.multiple_of(nearest(z, s) * span, LANES), span)
-        return pltpu.make_async_copy(outv.at[s], out_hbm.at[:, cols], out_sem.at[s])
-
     def close(s):
         share(s).wait_recv()
-        outv[s] = (own[s] + precv[s].astype(jnp.float32)).astype(jnp.bfloat16)
-        emit(s).start()
-
-    far_step("oa", 0, 0)
+        cols = pl.ds(pl.multiple_of(nearest(z, s) * span, LANES), span)
+        out_ref[:, cols] = (own[s] + precv[s].astype(jnp.float32)).astype(jnp.bfloat16)
+
+    def own_first(i, carry):
+        stretches(0, i, Z_LINE)
+        sibling_arrived(("a", "b"), 0, i)
+        normalize(0, nearest(z, i), inv_own)
+        project(0, 0, nearest(z, i))
+        return carry
+
+    lax.fori_loop(0, Z_LINE, own_first, 0)
+    local(cos_hbm, cos_ref, 7).wait()
+    local(sin_hbm, sin_ref, 8).wait()
+    stretch(4)
+    attend(0, 0)
+    stretch(5)
+    swap(hid_hbm, hid.at[1], 8, 6).wait_recv()
+    inv_other = inverse_rms(1)
+
+    def other_first(i, carry):
+        stretches(6, i, Z_LINE)
+        normalize(1, i, inv_other)
+        project(1, 0, i)
+        return carry
+
+    lax.fori_loop(0, Z_LINE, other_first, 0)
+    stretch(10)
+    attend(0, 1)
+
+    def other_second(i, carry):
+        stretches(11, i, Z_LINE)
+        sibling_arrived(("a", "b"), 1, i)
+        project(1, 1, nearest(z, i))
+        return carry
+
+    lax.fori_loop(0, Z_LINE, other_second, 0)
+    stretch(15)
+    attend(1, 1)
+    stretch(16)
     sibling_arrived(("oa", "ob"), 0, 0)
     out_other(0)
-    near_step("oa", "ob", 0, 1)
+
+    def own_second(i, carry):
+        stretches(17, i, Z_LINE)
+        project(0, 1, i)
+        return carry
+
+    lax.fori_loop(0, Z_LINE, own_second, 0)
+    stretch(21)
+    sibling_arrived(("oa", "ob"), 0, 1)
+    out_other(1)
+    stretch(22)
     attend(1, 0)
-    out_own(0)
 
     def out_step(s, carry):
-        far_step("oa", 0, s)
-
-        @pl.when(s < Z_LINE - 1)
-        def _():
-            near_step("oa", "ob", 0, s + 1)
-
-        sibling_arrived(("oa", "ob"), 0, s)
-        out_other(s)
+        for number in range(2):
+            stretch(23 + 2 * number, s == number)
         out_own(s)
-        return carry
-
-    lax.fori_loop(1, Z_LINE, out_step, 0)
+        for number in range(2):
+            stretch(24 + 2 * number, s == number)
+        sibling_arrived(("oa", "ob"), 0, s + 2)
+        out_other(s + 2)
+        return carry
+
+    lax.fori_loop(0, 2, out_step, 0)
+    for number in range(27, len(EDGE_PLAN)):
+        stretch(number)
+
+    def out_last(s, carry):
+        out_own(s)
+        return carry
+
+    lax.fori_loop(2, Z_LINE, out_last, 0)
+
+    for copy in swaps:
+        copy.wait_send()
+    for xs in range(2):
+        for g in range(GROUPS):
+            origin_ways(("a", "b"), g, xs, finish, middle)
+        origin_ways(("oa", "ob"), 0, xs, finish, middle)
+
+    def drain(k, carry):
+        for kind, g in PIECES:
+            sent(kind, g, k)
+        return carry
+
+    lax.fori_loop(0, Z_LINE, drain, 0)
 
     def close_step(s, carry):
         close(s)
+        share(s).wait_send()
         return carry
 
     lax.fori_loop(0, Z_LINE, close_step, 0)
-
-    for copy in swaps:
-        copy.wait_send()
-    for g in range(GROUPS):
-        for xs in range(2):
-            spread_origin(("a", "b"), g, xs, finish)
-    for xs in range(2):
-        spread_origin(("oa", "ob"), 0, xs, finish)
-
-    def drain_qkv(n, carry):
-        near_done("a", "b", n // Z_LINE, n % Z_LINE)
-        return carry
-
-    lax.fori_loop(0, steps, drain_qkv, 0)
-
-    def drain_out(s, carry):
-        near_done("oa", "ob", 0, s)
-        share(s).wait_send()
-        emit(s).wait()
-        return carry
-
-    lax.fori_loop(0, Z_LINE, drain_out, 0)
 
 
 def fused(hidden, attn_gain, w_query, w_key, w_value, w_out):
@@ -489,7 +558,6 @@
     qw, kw = width_query // 2 // GROUPS, width_kv // 2 // GROUPS
     half_out = width_query // 2
     span = width // Z_LINE
-    gain = jnp.broadcast_to(jnp.concatenate([attn_gain, attn_gain])[None, :], (16, LANES))
     cos_table, sin_table = lane_tables(tokens)
     kinds = 2 * GROUPS + 2
     dma = pltpu.SemaphoreType.DMA
@@ -497,11 +565,12 @@
         block_kernel,
         out_shape=jax.ShapeDtypeStruct((tokens, width), hidden.dtype),
         in_specs=[pl.BlockSpec(memory_space=pl.ANY)] * 8,
-        out_specs=pl.BlockSpec(memory_space=pl.ANY),
+        out_specs=pl.BlockSpec(memory_space=pltpu.VMEM),
         scratch_shapes=[
             pltpu.VMEM((GROUPS, fsdp, 2, 2, rows, qw + kw), jnp.bfloat16),
             pltpu.VMEM((GROUPS, fsdp, 2, 2, rows + 16, kw), jnp.bfloat16),
-            pltpu.VMEM((fsdp, 2, 2, rows, half_out), jnp.bfloat16),
+            pltpu.VMEM((fsdp, 2, 2, rows, half_out - LANES), jnp.bfloat16),
+            pltpu.VMEM((fsdp, 2, 2, rows, LANES), jnp.bfloat16),
             pltpu.VMEM((2, tokens, width), jnp.bfloat16),
             pltpu.VMEM((2 * tokens, width), jnp.bfloat16),
             pltpu.VMEM((GROUPS, 2 * tokens, qw + 2 * kw), jnp.float32),
@@ -511,22 +580,24 @@
             pltpu.VMEM((Z_LINE, tokens, span), jnp.bfloat16),
             pltpu.VMEM((Z_LINE, tokens, span), jnp.bfloat16),
             pltpu.VMEM((Z_LINE, tokens, span), jnp.float32),
-            pltpu.VMEM((Z_LINE, tokens, span), jnp.bfloat16),
+            pltpu.VMEM((1, rows), jnp.bfloat16),
+            pltpu.VMEM((16, LANES), jnp.bfloat16),
             dma((kinds, 2, 4)),
             dma((kinds, fsdp, 4)),
             dma((kinds, fsdp)),
             dma((kinds, fsdp)),
+            dma((11,)),
+            dma((7,)),
             dma((10,)),
-            dma((6,)),
-            dma((8,)),
-            dma((Z_LINE,)),
             dma((Z_LINE,)),
             dma((Z_LINE,)),
         ],
         compiler_params=pltpu.CompilerParams(
-            collective_id=0, has_side_effects=True, vmem_limit_bytes=60 * 1024 * 1024),
+            collective_id=0, has_side_effects=True, vmem_limit_bytes=40 * 1024 * 1024),
         name="attention_block",
-    )(hidden, gain, w_query, w_key, w_value, w_out.T, jnp.asarray(cos_table), jnp.asarray(sin_table))
+    )(*[pltpu.with_memory_space_constraint(value, pltpu.HBM) for value in (
+        hidden, attn_gain[None, :], w_query, w_key, w_value, w_out.T,
+        jnp.asarray(cos_table), jnp.asarray(sin_table))])
 
 
 def fits(fsdp, rep, hidden, w_query, w_key, w_out):

time: 94.2 us -> 77.8 us (0.83)
  Pallas kernels: 90.4 us -> 76.6 us
  local copies, waits for them, and re-layouts: 3.56 us -> 0.97 us
    pallas_call x1, Pallas kernels: 90.4 us -> 76.6 us  [fused(): pl.pallas_call(block_kernel, out_shape=jax.ShapeDtypeStruct((tokens, widt...]
    unnamed x3 -> x1, local copies, waits for them, and re-layouts: 2.96 us -> 0.97 us
where the time goes in v2:
time: 77.8 us; the launch traced here: 77.6 us
  Pallas kernels  76.6 us (98%)
  local copies, waits for them, and re-layouts  0.97 us (1%)
    pallas_call x1, Pallas kernels, fused(): pl.pallas_call(block_kernel, out_shape=jax.ShapeDtypeStruct((tokens, widt...  76.6 us

profile of v2, /device:TPU:0, one launch (start us, length us, event | category | flops | bytes accessed | tf_op | source)
XLA Modules:
  0.0 77.6 jit_solution(16349575133687630075)
XLA Ops:
  0.0 76.6 %attention_block.1 = bf16[256,2048]{1,0:T(8,128)(2,1)S(1)} custom-call(bf16[256,2048]{1,0:T(8,128)(2,1)} %hid_hbm.1, bf16[1,64]{1,0:T(2,128)(2,1)} %bitcast.3, bf16[64,2048]{1,0:T(8,128)(2,1)} %wq_hbm.1, bf16[64,512]{1,0:T(8,128)(2,1)} %wk_hbm.1, bf16[64,512]{1,0:T(8,128)(2,1)} %wv_hbm.1, bf16[64,2048]{1,0:T(8,128)(2,1)} %bitcast.2, ...), custom_call_target="tpu_custom_call" | custom-call | tf_op jit(solution)/shard_map/attention_block/pallas_call | solution.py:564
  76.7 1.0 %copy.10 = bf16[256,2048]{1,0:T(8,128)(2,1)} copy(bf16[256,2048]{1,0:T(8,128)(2,1)S(1)} %attention_block.1) | data formatting | bytes 2097152

commit v3 on v2

--- a/solution.py
+++ b/solution.py
@@ -18,36 +18,46 @@
 
 MESH = pl.DeviceIdType.MESH
 NT = (((1,), (1,)), ((), ()))
-
+TN = (((0,), (0,)), ((), ()))
+
+BUFFERS = ("a", "b", "oa", "ob")
 PIECES = (("a", 0), ("a", 1), ("b", 0), ("b", 1), ("oa", 0), ("ob", 0))
 EDGE_PLAN = (
-    (100, 102, 101, 103, 1, 20, 9, 17, 28, 2, 4, 5, 13, 3, 22,),
-    (21, 26, 18, 12, 6,),
-    (25, 104, 7, 19,),
-    (23,),
+    (102, 100, 101, 103, 20, 1, 4, 28, 17, 104, 2, 3, 21, 9, 23, 22,),
+    (25, 18, 12, 19, 6, 7, 5,),
     (10,),
     (),
     (),
-    (11, 29,),
-    (27, 105, 14,),
-    (),
-    (),
-    (30, 15,),
+    (),
+    (),
+    (11, 13,),
+    (),
+    (14, 27, 29, 105,),
     (31,),
-    (),
-    (36,),
-    (44, 33,),
-    (),
-    (34, 41,),
-    (45, 37,),
-    (),
-    (),
-    (),
-    (),
-    (35, 38, 46,),
+    (30, 26, 15,),
+    (),
+    (),
+    (),
+    (),
+    (),
+    (33, 36, 44,),
+    (),
+    (41,),
+    (),
+    (),
+    (),
+    (34, 37, 45,),
     (42,),
+    (),
+    (35,),
+    (46, 38,),
+    (43,),
     (47,),
-    (43, 39,),
+    (39,),
+    (),
+    (),
+    (),
+    (),
     (),
     (),
     (),
@@ -57,33 +67,41 @@
     (),
 )
 MIDDLE_PLAN = (
-    (100, 102, 101, 103, 0, 21, 16, 5, 18, 2, 20, 3, 24, 23,),
-    (13, 6, 22, 26, 19, 4, 8, 10,),
-    (),
-    (28, 7,),
-    (11,),
-    (27, 12, 29, 14,),
+    (102, 100, 101, 103, 0, 16, 21, 2, 5, 28, 20, 29, 4, 3, 6, 24, 23, 8, 22,),
+    (19, 18, 7, 10, 11, 27, 26, 31, 12, 13,),
+    (),
+    (),
+    (),
+    (30,),
     (104,),
     (),
     (),
-    (30, 31, 105,),
+    (14,),
+    (105,),
     (),
     (15,),
     (),
+    (),
     (32, 34,),
-    (37, 45,),
-    (),
-    (40,),
-    (44,),
-    (),
-    (35,),
-    (46, 36,),
-    (42,),
-    (),
-    (47, 43, 38,),
-    (),
-    (),
-    (39,),
+    (),
+    (45, 37, 40,),
+    (),
+    (),
+    (),
+    (42, 36, 44, 35,),
+    (46,),
+    (),
+    (43,),
+    (),
+    (38,),
+    (),
+    (),
+    (),
+    (),
+    (39, 47,),
+    (),
+    (),
+    (),
     (),
     (),
     (),
@@ -127,10 +145,10 @@
 
 
 def block_kernel(
-    hid_hbm, gain_hbm, wq_hbm, wk_hbm, wv_hbm, wo_hbm, cos_hbm, sin_hbm, out_ref,
-    wa, wv, woa, wob, hid, nrm, acc, ctx, cos_ref, sin_ref, psend, precv, own, gain_in, gain_tile,
-    origin_sem, send_sem, recv_sem, sib_sem, xsend_sem, xrecv_sem, local_sem,
-    psend_sem, precv_sem,
+    hid_hbm, gain_hbm, wq_hbm, wk_hbm, wv_hbm, wo_hbm, cos_hbm, sin_hbm, own_out, other_out,
+    wa, wv, woa, wob, hid, nrm, acc, ctx, cos_ref, sin_ref, psend, own, gain_in, gain_tile,
+    send_sem, recv_sem, sib_sem, sibo_sem, xsend_sem, xrecv_sem, local_sem,
+    psend_sem, precv_sem, own_sem,
 ):
     f, r = lax.axis_index("fsdp"), lax.axis_index("rep")
     z, y = f // 2, f % 2
@@ -142,6 +160,7 @@
     cut = woa.shape[4]
     half_out = cut + wob.shape[4]
     span = width // Z_LINE
+    piece_cols = 4 * rows
     partner = (f, (1 - x) * 2 + c)
     sibling = (f, x * 2 + 1 - c)
     across = (z * 2 + 1 - y, r)
@@ -171,23 +190,28 @@
     targets = {"outward": (0, outward), "inward": (1, inward), "across": (2, across),
                "sibling": (3, sibling)}
 
+    def arrival(kind, k, fs, way):
+        if way != "sibling":
+            return recv_sem.at[k, fs]
+        if kind in ("a", "b"):
+            return sib_sem.at[k, fs // 2]
+        return sibo_sem.at[k - 2 * GROUPS, fs]
+
     def remote(kind, g, fs, way):
         number, target = targets[way]
         k = index(kind, g)
         ref = view(kind, g, fs, c)
-        arrive = sib_sem if way == "sibling" else recv_sem
         return pltpu.make_async_remote_copy(
-            src_ref=ref, dst_ref=ref, send_sem=send_sem.at[k, fs, number],
-            recv_sem=arrive.at[k, fs], device_id=target, device_id_type=MESH)
+            src_ref=ref, dst_ref=ref, send_sem=send_sem.at[BUFFERS.index(kind), number],
+            recv_sem=arrival(kind, k, fs, way), device_id=target, device_id_type=MESH)
 
     def origin(kind, g, xs, way):
         number, target = targets[way]
         k = index(kind, g)
         ref = view(kind, g, f, c).at[xs]
-        arrive = sib_sem if way == "sibling" else recv_sem
         return pltpu.make_async_remote_copy(
-            src_ref=ref, dst_ref=ref, send_sem=origin_sem.at[k, xs, number],
-            recv_sem=arrive.at[k, f], device_id=target, device_id_type=MESH)
+            src_ref=ref, dst_ref=ref, send_sem=send_sem.at[BUFFERS.index(kind), number],
+            recv_sem=arrival(kind, k, f, way), device_id=target, device_id_type=MESH)
 
     def relay(piece, own):
         kind, g = PIECES[piece // 8]
@@ -204,49 +228,31 @@
                 remote(kind, g, fs, "across").start()
         remote(kind, g, fs, "sibling").start()
 
-    def sent(kind, g, k):
-        main = kind in ("a", "oa")
-        out_ok, in_ok = middle & (k >= mine), k <= mine
-
-        def column(col, side):
-            fs = at_line(k) * 2 + (y if col == 0 else 1 - y)
-            if side:
-                pl.when(out_ok)(lambda: remote(kind, g, fs, "outward").wait_send())
-                pl.when(in_ok)(lambda: remote(kind, g, fs, "inward").wait_send())
-            if main and col == 0:
-                remote(kind, g, fs, "across").wait_send()
-            remote(kind, g, fs, "sibling").wait_send()
-
-        pl.when(k != mine)(lambda: column(0, True))
-        column(1, not main)
-
-    def origin_ways(kinds, g, xs, act, middle_chip):
+    def sent(way, main_count, side_count):
+        number, target = targets[way]
+        for buffer, kind in enumerate(BUFFERS):
+            count = pl.ds(0, main_count if kind in ("a", "oa") else side_count)
+            ref = {"a": lambda: wa.at[:, count, :, c], "b": lambda: wv.at[:, count, :, c],
+                   "oa": lambda: woa.at[count, :, c], "ob": lambda: wob.at[count, :, c]}[kind]()
+            pltpu.make_async_remote_copy(
+                src_ref=ref, dst_ref=ref, send_sem=send_sem.at[buffer, number],
+                recv_sem=recv_sem.at[0, 0], device_id=target, device_id_type=MESH).wait_send()
+
+    def origin_ways(kinds, g, xs, own):
         for kind in kinds:
             for way in targets:
-                if way == "outward":
-                    if middle_chip is True:
-                        act(origin(kind, g, xs, way))
-                    elif middle_chip is not False:
-                        pl.when(middle_chip)(lambda kind=kind: act(origin(kind, g, xs, "outward")))
-                else:
-                    act(origin(kind, g, xs, way))
-
-    def start(copy):
-        copy.start()
-
-    def finish(copy):
-        copy.wait_send()
+                if way != "outward" or own > 0:
+                    origin(kind, g, xs, way).start()
 
     def sibling_arrived(kinds, g, s):
         zs = nearest(z, s)
+        both = pl.ds(zs * 2, 2)
         for kind in kinds:
-            for col in range(2):
-                fs = zs * 2 + col
-                ref = view(kind, g, fs, 1 - c)
-                pltpu.make_async_remote_copy(
-                    src_ref=ref, dst_ref=ref, send_sem=send_sem.at[index(kind, g), fs, 3],
-                    recv_sem=sib_sem.at[index(kind, g), fs], device_id=sibling,
-                    device_id_type=MESH).wait_recv()
+            ref = view(kind, g, both, 1 - c)
+            pltpu.make_async_remote_copy(
+                src_ref=ref, dst_ref=ref, send_sem=send_sem.at[0, 3],
+                recv_sem=sib_sem.at[index(kind, g), zs], device_id=sibling,
+                device_id_type=MESH).wait_recv()
 
     def q_cols(h, g):
         return pl.ds(pl.multiple_of((h * GROUPS + g) * qw, LANES), qw)
@@ -303,14 +309,14 @@
     for g in range(GROUPS):
         h = 1 - x
         swaps += [
-            swap(wq_hbm.at[:, q_cols(h, g)], wa.at[g, f, x, c, :, pl.ds(0, qw)], 4 * g, 2 * g),
-            swap(wk_hbm.at[:, k_cols(h, g)], wa.at[g, f, x, c, :, pl.ds(qw, kw)], 4 * g + 1, 2 * g),
-            swap(wv_hbm.at[:, k_cols(h, g)], wv.at[g, f, x, c, pl.ds(0, rows)], 4 * g + 2, 2 * g + 1),
-            swap(gain_tile, wv.at[g, f, x, c, pl.ds(rows, 16)], 4 * g + 3, 2 * g + 1),
+            swap(wq_hbm.at[:, q_cols(h, g)], wa.at[g, f, x, c, :, pl.ds(0, qw)], 0, 2 * g),
+            swap(wk_hbm.at[:, k_cols(h, g)], wa.at[g, f, x, c, :, pl.ds(qw, kw)], 0, 2 * g),
+            swap(wv_hbm.at[:, k_cols(h, g)], wv.at[g, f, x, c, pl.ds(0, rows)], 1, 2 * g + 1),
+            swap(gain_tile, wv.at[g, f, x, c, pl.ds(rows, 16)], 1, 2 * g + 1),
         ]
-    swaps.append(swap(hid_hbm, hid.at[1], 8, 6))
-    swaps.append(swap(wo_hbm.at[:, oa_cols(1 - x)], woa.at[f, x, c], 9, 4))
-    swaps.append(swap(wo_hbm.at[:, ob_cols(1 - x)], wob.at[f, x, c], 10, 5))
+    swaps.append(swap(hid_hbm, hid.at[1], 2, 6))
+    swaps.append(swap(wo_hbm.at[:, oa_cols(1 - x)], woa.at[f, x, c], 3, 4))
+    swaps.append(swap(wo_hbm.at[:, ob_cols(1 - x)], wob.at[f, x, c], 4, 5))
     for copy in swaps:
         copy.start()
 
@@ -341,8 +347,7 @@
                             stage, xs = (code - 100) // 2, (code - 100) % 2
                             ready(stage, xs)
                             kinds = ("a", "b") if stage < GROUPS else ("oa", "ob")
-                            origin_ways(kinds, stage % GROUPS, x if xs == 0 else 1 - x, start,
-                                        own == 1)
+                            origin_ways(kinds, stage % GROUPS, x if xs == 0 else 1 - x, own)
                 pl.when(here if cond is None else here & cond)(run)
 
     def stretches(first, step, count):
@@ -388,6 +393,11 @@
         key = turn(acc[g, span_rows, qw:qw + kw])
         value = acc[g, span_rows, qw + kw:qw + 2 * kw]
         key_other, value_other = pltpu.roll(key, HD, 1), pltpu.roll(value, HD, 1)
+        heads = qw // (kw // HD)
+        block = tokens // 2
+        wide = heads // LANES * block
+        key_at = lax.broadcasted_iota(jnp.int32, (block, wide), 0)
+        open_ = lax.broadcasted_iota(jnp.int32, (block, wide), 1) % block >= key_at
         for j in range(kw // HD):
             def low_high(tile, tile_other):
                 low = tile if j == 0 else tile_other
@@ -398,64 +408,67 @@
 
             key_low, key_high = low_high(key, key_other)
             value_low, value_high = low_high(value, value_other)
-            heads = qw // (kw // HD)
             query = []
             for p in range(heads // LANES):
                 at = j * heads + p * LANES
                 tile = turn(acc[g, span_rows, at:at + LANES])
                 query.append(tile.astype(jnp.bfloat16) * jnp.bfloat16(HD ** -0.5))
-            block = tokens // 2
             for b in range(2):
                 seen = (b + 1) * block
-                rows_q = slice(b * block, (b + 1) * block)
-                stacked = jnp.concatenate([q[rows_q] for q in query], axis=0)
+                stacked = jnp.concatenate([q[b * block:seen] for q in query], axis=0)
                 keys = jnp.concatenate([key_low[:seen], key_high[:seen]], axis=0)
                 values = jnp.concatenate([value_low[:seen], value_high[:seen]], axis=0)
-                scores = lax.dot_general(stacked, keys, NT, preferred_element_type=jnp.float32)
-                count = stacked.shape[0]
-                at_row = lax.broadcasted_iota(jnp.int32, (count, seen), 0) % block + b * block
-                at_col = lax.broadcasted_iota(jnp.int32, (count, seen), 1)
-                open_ = at_row >= at_col
+                scores = lax.dot_general(keys, stacked, NT, preferred_element_type=jnp.float32)
                 probs = []
                 for e in range(2):
-                    part = jnp.where(open_, scores[:, e * seen:(e + 1) * seen], -1e30)
-                    top = jnp.max(part, axis=-1, keepdims=True)
-                    expo = jnp.exp(part - top)
-                    total = jnp.sum(expo, axis=-1, keepdims=True)
+                    begin, end = e * seen, (e + 1) * seen
+                    part = jnp.where(open_, scores[end - block:end], -1e30)
+                    if b > 0:
+                        part = jnp.concatenate([scores[begin:end - block], part], axis=0)
+                    expo = jnp.exp(part - jnp.max(part, axis=0, keepdims=True))
+                    total = jnp.sum(expo, axis=0, keepdims=True)
                     probs.append((expo * (1.0 / total)).astype(jnp.bfloat16))
-                mixed = jnp.dot(jnp.concatenate(probs, axis=1), values,
-                                preferred_element_type=jnp.float32).astype(jnp.bfloat16)
+                mixed = lax.dot_general(jnp.concatenate(probs, axis=0), values, TN,
+                                        preferred_element_type=jnp.float32).astype(jnp.bfloat16)
                 for p in range(heads // LANES):
                     at = g * qw + j * heads + p * LANES
                     ctx[pl.ds(base + b * block, block), at:at + LANES] = (
                         mixed[p * block:(p + 1) * block])
 
-    def out_weight(s):
-        fs = pl.ds(nearest(z, s) * 2, 2)
-        return jnp.concatenate(
-            [woa[fs].reshape(span, cut), wob[fs].reshape(span, half_out - cut)], axis=1)
-
-    def share(s):
-        return pltpu.make_async_remote_copy(
-            src_ref=psend.at[s], dst_ref=precv.at[s], send_sem=psend_sem.at[s],
-            recv_sem=precv_sem.at[s], device_id=partner, device_id_type=MESH)
-
-    def out_other(s):
-        part = lax.dot_general(ctx[tokens:2 * tokens, :], out_weight(s), NT,
+    def place(s, col):
+        return nearest(z, s) * 2 + (y if col == 0 else 1 - y)
+
+    def block_cols(fs):
+        return pl.ds(pl.multiple_of(fs * piece_cols, LANES), piece_cols)
+
+    def out_part(fs):
+        weight = jnp.concatenate([woa[fs].reshape(piece_cols, cut),
+                                  wob[fs].reshape(piece_cols, half_out - cut)], axis=1)
+        return lax.dot_general(ctx[tokens:2 * tokens, :], weight, NT,
                                preferred_element_type=jnp.float32)
-        psend[s] = part.astype(jnp.bfloat16)
-        share(s).start()
+
+    def out_other(s, col):
+        fs = place(s, col)
+        for kind in ("oa", "ob"):
+            ref = view(kind, 0, fs, 1 - c)
+            pltpu.make_async_remote_copy(
+                src_ref=ref, dst_ref=ref, send_sem=send_sem.at[0, 3],
+                recv_sem=sibo_sem.at[index(kind, 0) - 2 * GROUPS, fs], device_id=sibling,
+                device_id_type=MESH).wait_recv()
+        psend[fs] = out_part(fs).astype(jnp.bfloat16)
+        pltpu.make_async_remote_copy(
+            src_ref=psend.at[fs], dst_ref=other_out.at[:, block_cols(fs)], send_sem=psend_sem,
+            recv_sem=precv_sem, device_id=partner, device_id_type=MESH).start()
 
     def out_own(s):
-        cols = pl.ds(pl.multiple_of(nearest(z, s) * span, LANES), span)
-        part = lax.dot_general(ctx[0:tokens, :], out_weight(s), NT,
-                               preferred_element_type=jnp.float32)
-        own[s] = hid[0, :, cols].astype(jnp.float32) + part
-
-    def close(s):
-        share(s).wait_recv()
-        cols = pl.ds(pl.multiple_of(nearest(z, s) * span, LANES), span)
-        out_ref[:, cols] = (own[s] + precv[s].astype(jnp.float32)).astype(jnp.bfloat16)
+        zs = nearest(z, s)
+        both = pl.ds(zs * 2, 2)
+        weight = jnp.concatenate([woa[both].reshape(span, cut),
+                                  wob[both].reshape(span, half_out - cut)], axis=1)
+        part = lax.dot_general(ctx[0:tokens, :], weight, NT, preferred_element_type=jnp.float32)
+        cols = pl.ds(pl.multiple_of(zs * span, LANES), span)
+        own[zs] = hid[0, :, cols].astype(jnp.float32) + part
+        pltpu.make_async_copy(own.at[zs], own_out.at[:, cols], own_sem).start()
 
     def own_first(i, carry):
         stretches(0, i, Z_LINE)
@@ -470,7 +483,7 @@
     stretch(4)
     attend(0, 0)
     stretch(5)
-    swap(hid_hbm, hid.at[1], 8, 6).wait_recv()
+    swap(hid_hbm, hid.at[1], 2, 6).wait_recv()
     inv_other = inverse_rms(1)
 
     def other_first(i, carry):
@@ -493,61 +506,59 @@
     stretch(15)
     attend(1, 1)
     stretch(16)
-    sibling_arrived(("oa", "ob"), 0, 0)
-    out_other(0)
+    out_other(0, 0)
+    stretch(17)
+    out_other(0, 1)
 
     def own_second(i, carry):
-        stretches(17, i, Z_LINE)
+        stretches(18, i, Z_LINE)
         project(0, 1, i)
         return carry
 
     lax.fori_loop(0, Z_LINE, own_second, 0)
-    stretch(21)
-    sibling_arrived(("oa", "ob"), 0, 1)
-    out_other(1)
     stretch(22)
+    out_other(1, 0)
+    stretch(23)
+    out_other(1, 1)
+    stretch(24)
     attend(1, 0)
-
-    def out_step(s, carry):
-        for number in range(2):
-            stretch(23 + 2 * number, s == number)
-        out_own(s)
-        for number in range(2):
-            stretch(24 + 2 * number, s == number)
-        sibling_arrived(("oa", "ob"), 0, s + 2)
-        out_other(s + 2)
-        return carry
-
-    lax.fori_loop(0, 2, out_step, 0)
-    for number in range(27, len(EDGE_PLAN)):
+    stretch(25)
+    out_other(2, 0)
+    stretch(26)
+    out_own(0)
+    stretch(27)
+    out_other(2, 1)
+    stretch(28)
+    out_own(1)
+    stretch(29)
+    out_other(3, 0)
+    stretch(30)
+    out_own(2)
+    stretch(31)
+    out_other(3, 1)
+    stretch(32)
+    out_own(3)
+    for number in range(33, len(EDGE_PLAN)):
         stretch(number)
 
-    def out_last(s, carry):
-        out_own(s)
-        return carry
-
-    lax.fori_loop(2, Z_LINE, out_last, 0)
-
-    for copy in swaps:
-        copy.wait_send()
-    for xs in range(2):
-        for g in range(GROUPS):
-            origin_ways(("a", "b"), g, xs, finish, middle)
-        origin_ways(("oa", "ob"), 0, xs, finish, middle)
-
-    def drain(k, carry):
-        for kind, g in PIECES:
-            sent(kind, g, k)
-        return carry
-
-    lax.fori_loop(0, Z_LINE, drain, 0)
-
-    def close_step(s, carry):
-        close(s)
-        share(s).wait_send()
-        return carry
-
-    lax.fori_loop(0, Z_LINE, close_step, 0)
+    for number, ref in enumerate((wa.at[:, f, 0, c], wv.at[:, f, 0, c], hid.at[1],
+                                  woa.at[f, 0, c], wob.at[f, 0, c])):
+        swap(ref, ref, number, 0).wait_send()
+    sent("sibling", 2 * Z_LINE, 2 * Z_LINE)
+    sent("across", Z_LINE, 1)
+    pl.when(edge)(lambda: sent("inward", 1, 2))
+
+    @pl.when(middle)
+    def _():
+        sent("inward", 2, 4)
+        sent("outward", 3, 6)
+
+    pltpu.make_async_copy(own, own, own_sem).wait()
+    everything = pltpu.make_async_remote_copy(
+        src_ref=psend, dst_ref=psend, send_sem=psend_sem, recv_sem=precv_sem, device_id=partner,
+        device_id_type=MESH)
+    everything.wait_send()
+    everything.wait_recv()
 
 
 def fused(hidden, attn_gain, w_query, w_key, w_value, w_out):
@@ -561,11 +572,12 @@
     cos_table, sin_table = lane_tables(tokens)
     kinds = 2 * GROUPS + 2
     dma = pltpu.SemaphoreType.DMA
-    return pl.pallas_call(
+    own, other = pl.pallas_call(
         block_kernel,
-        out_shape=jax.ShapeDtypeStruct((tokens, width), hidden.dtype),
+        out_shape=(jax.ShapeDtypeStruct((tokens, width), jnp.float32),
+                   jax.ShapeDtypeStruct((tokens, width), jnp.bfloat16)),
         in_specs=[pl.BlockSpec(memory_space=pl.ANY)] * 8,
-        out_specs=pl.BlockSpec(memory_space=pltpu.VMEM),
+        out_specs=(pl.BlockSpec(memory_space=pl.ANY), pl.BlockSpec(memory_space=pl.ANY)),
         scratch_shapes=[
             pltpu.VMEM((GROUPS, fsdp, 2, 2, rows, qw + kw), jnp.bfloat16),
             pltpu.VMEM((GROUPS, fsdp, 2, 2, rows + 16, kw), jnp.bfloat16),
@@ -577,20 +589,20 @@
             pltpu.VMEM((2 * tokens, half_out), jnp.bfloat16),
             pltpu.VMEM((tokens, LANES), jnp.float32),
             pltpu.VMEM((tokens, LANES), jnp.float32),
-            pltpu.VMEM((Z_LINE, tokens, span), jnp.bfloat16),
-            pltpu.VMEM((Z_LINE, tokens, span), jnp.bfloat16),
+            pltpu.VMEM((fsdp, tokens, 4 * rows), jnp.bfloat16),
             pltpu.VMEM((Z_LINE, tokens, span), jnp.float32),
             pltpu.VMEM((1, rows), jnp.bfloat16),
             pltpu.VMEM((16, LANES), jnp.bfloat16),
-            dma((kinds, 2, 4)),
-            dma((kinds, fsdp, 4)),
+            dma((len(BUFFERS), 4)),
             dma((kinds, fsdp)),
-            dma((kinds, fsdp)),
-            dma((11,)),
+            dma((2 * GROUPS, Z_LINE)),
+            dma((2, fsdp)),
+            dma((5,)),
             dma((7,)),
             dma((10,)),
-            dma((Z_LINE,)),
-            dma((Z_LINE,)),
+            dma,
+            dma,
+            dma,
         ],
         compiler_params=pltpu.CompilerParams(
             collective_id=0, has_side_effects=True, vmem_limit_bytes=40 * 1024 * 1024),
@@ -598,6 +610,7 @@
     )(*[pltpu.with_memory_space_constraint(value, pltpu.HBM) for value in (
         hidden, attn_gain[None, :], w_query, w_key, w_value, w_out.T,
         jnp.asarray(cos_table), jnp.asarray(sin_table))])
+    return (own + other.astype(jnp.float32)).astype(hidden.dtype)
 
 
 def fits(fsdp, rep, hidden, w_query, w_key, w_out):

time: 77.8 us -> 73.5 us (0.945)
  Pallas kernels: 76.6 us -> 72.1 us
  other arithmetic: 0 us -> 1.26 us
  local copies, waits for them, and re-layouts: 0.97 us -> 0 us
    pallas_call x1, Pallas kernels: 76.6 us -> 72.1 us  [fused(): pl.pallas_call(block_kernel, out_shape=(jax.ShapeDtypeStruct((tokens, wid...]
    convert_element_type x0 -> x1, other arithmetic: none -> 1.26 us  [fused(): return (own + other.astype(jnp.float32)).astype(hidden.dtype)]
    unnamed x1 -> x0, local copies, waits for them, and re-layouts: 0.97 us -> none
where the time goes in v3:
time: 73.5 us; the launch traced here: 73.3 us
  Pallas kernels  72.1 us (98%)
  other arithmetic  1.26 us (2%)
    pallas_call x1, Pallas kernels, fused(): pl.pallas_call(block_kernel, out_shape=(jax.ShapeDtypeStruct((tokens, wid...  72.1 us

profile of v3, /device:TPU:0, one launch (start us, length us, event | category | flops | bytes accessed | tf_op | source)
XLA Modules:
  0.0 73.3 jit_solution(1186783108033628666)
XLA Ops:
  0.0 72.1 %attention_block.1 = (f32[256,2048]{1,0:T(8,128)S(1)}, bf16[256,2048]{1,0:T(8,128)(2,1)S(1)}) custom-call(bf16[256,2048]{1,0:T(8,128)(2,1)} %hid_hbm.1, bf16[1,64]{1,0:T(2,128)(2,1)} %bitcast.3, bf16[64,2048]{1,0:T(8,128)(2,1)} %wq_hbm.1, bf16[64,512]{1,0:T(8,128)(2,1)} %wk_hbm.1, bf16[64,512]{1,0:T(8,128)(2,1)} %wv_hbm.1, bf16[64,2048]{1,0:T(8,128)(2,1)} %bitcast.2, ...), custom_call_target="tpu_custom_call" | custom-call | tf_op jit(solution)/shard_map/attention_block/pallas_call | solution.py:575
  72.1 1.3 %add_convert_fusion = bf16[256,2048]{1,0:T(8,128)(2,1)} fusion(f32[256,2048]{1,0:T(8,128)S(1)} %get-tuple-element.7, bf16[256,2048]{1,0:T(8,128)(2,1)S(1)} %get-tuple-element.8), kind=kLoop, calls=%fused_computation | loop fusion | flops 1572864 | bytes 4194304 | tf_op jit(solution)/shard_map/convert_element_type | solution.py:613

commit v4 on v3

--- a/solution.py
+++ b/solution.py
@@ -23,35 +23,36 @@
 BUFFERS = ("a", "b", "oa", "ob")
 PIECES = (("a", 0), ("a", 1), ("b", 0), ("b", 1), ("oa", 0), ("ob", 0))
 EDGE_PLAN = (
-    (102, 100, 101, 103, 20, 1, 4, 28, 17, 104, 2, 3, 21, 9, 23, 22,),
-    (25, 18, 12, 19, 6, 7, 5,),
+    (102, 100, 101, 103, 4, 1, 20, 25, 17,),
+    (18, 104, 28, 12, 2, 21, 5, 3, 9, 6, 22, 19, 23,),
+    (7, 11,),
+    (),
+    (),
     (10,),
-    (),
-    (),
-    (),
-    (),
-    (11, 13,),
-    (),
-    (14, 27, 29, 105,),
-    (31,),
-    (30, 26, 15,),
-    (),
-    (),
-    (),
-    (),
-    (),
-    (33, 36, 44,),
-    (),
-    (41,),
-    (),
-    (),
-    (),
-    (34, 37, 45,),
-    (42,),
-    (),
-    (35,),
-    (46, 38,),
-    (43,),
+    (13,),
+    (29, 27, 15,),
+    (),
+    (105, 31,),
+    (26,),
+    (30, 14,),
+    (),
+    (),
+    (),
+    (),
+    (),
+    (33, 41, 36, 44,),
+    (),
+    (),
+    (),
+    (),
+    (),
+    (34, 42, 45,),
+    (37,),
+    (),
+    (),
+    (35, 43,),
+    (38,),
+    (46,),
     (47,),
     (39,),
     (),
@@ -64,41 +65,40 @@
     (),
     (),
     (),
-    (),
 )
 MIDDLE_PLAN = (
-    (102, 100, 101, 103, 0, 16, 21, 2, 5, 28, 20, 29, 4, 3, 6, 24, 23, 8, 22,),
-    (19, 18, 7, 10, 11, 27, 26, 31, 12, 13,),
-    (),
-    (),
-    (),
+    (100, 102, 101, 103, 5, 0, 18, 16, 2, 21, 20, 13, 24, 3, 19,),
+    (4, 22, 8, 6, 23,),
+    (11, 7, 28,),
+    (10, 29, 27,),
+    (31,),
+    (),
+    (15, 12, 26,),
     (30,),
+    (),
     (104,),
-    (),
-    (),
-    (14,),
-    (105,),
-    (),
-    (15,),
-    (),
-    (),
-    (32, 34,),
-    (),
-    (45, 37, 40,),
-    (),
-    (),
-    (),
-    (42, 36, 44, 35,),
+    (14, 105,),
+    (),
+    (),
+    (),
+    (),
+    (),
+    (32,),
+    (34, 40, 42,),
+    (),
+    (37,),
+    (),
+    (),
+    (),
+    (44, 45, 35, 43,),
+    (36,),
+    (),
+    (),
+    (),
     (46,),
-    (),
-    (43,),
-    (),
-    (38,),
-    (),
-    (),
-    (),
-    (),
-    (39, 47,),
+    (38, 47, 39,),
+    (),
+    (),
     (),
     (),
     (),
@@ -110,6 +110,13 @@
     (),
     (),
 )
+FIRST_ORDER = ((0, 2, 1, 3), (1, 0, 3, 2))
+SECOND_ORDER = ((1, 3, 0, 2), (3, 0, 2, 1))
+OTHER_ORDER = (
+    ((0, 0), (0, 1), (1, 0), (0, 2), (1, 1), (0, 3), (1, 2), (1, 3)),
+    ((0, 1), (0, 0), (0, 2), (0, 3), (1, 0), (1, 1), (1, 3), (1, 2)),
+)
+OWN_ORDER = ((0, 1, 2, 3), (0, 1, 3, 2))
 
 
 def rope_tables(tokens, head_dim):
@@ -133,15 +140,6 @@
     angle = np.arange(tokens)[:, None] * freq[None, :]
     sign = np.where(lane % HD < HD // 2, -1.0, 1.0)
     return np.cos(angle).astype(np.float32), (np.sin(angle) * sign).astype(np.float32)
-
-
-def nearest(p, step):
-    middle = jnp.where((p == 1) | (p == 2), 1, 0)
-    high = step // 2
-    low = step % 2
-    low = low + middle * high * (1 - 2 * low)
-    first = (1 - 2 * (p % 2)) * low
-    return p + first + (2 - 4 * (p // 2)) * high
 
 
 def block_kernel(
@@ -190,6 +188,11 @@
     targets = {"outward": (0, outward), "inward": (1, inward), "across": (2, across),
                "sibling": (3, sibling)}
 
+    def picked(i, orders):
+        k = sum(jnp.where(i == j, jnp.where(edge, e, m), 0)
+                for j, (e, m) in enumerate(zip(*orders)))
+        return at_line(k)
+
     def arrival(kind, k, fs, way):
         if way != "sibling":
             return recv_sem.at[k, fs]
@@ -244,8 +247,7 @@
                 if way != "outward" or own > 0:
                     origin(kind, g, xs, way).start()
 
-    def sibling_arrived(kinds, g, s):
-        zs = nearest(z, s)
+    def sibling_arrived(kinds, g, zs):
         both = pl.ds(zs * 2, 2)
         for kind in kinds:
             ref = view(kind, g, both, 1 - c)
@@ -435,8 +437,10 @@
                     ctx[pl.ds(base + b * block, block), at:at + LANES] = (
                         mixed[p * block:(p + 1) * block])
 
-    def place(s, col):
-        return nearest(z, s) * 2 + (y if col == 0 else 1 - y)
+    def place(n):
+        col, k = (jnp.where(edge, OTHER_ORDER[0][n][which], OTHER_ORDER[1][n][which])
+                  for which in range(2))
+        return at_line(k) * 2 + jnp.where(col == 0, y, 1 - y)
 
     def block_cols(fs):
         return pl.ds(pl.multiple_of(fs * piece_cols, LANES), piece_cols)
@@ -447,8 +451,8 @@
         return lax.dot_general(ctx[tokens:2 * tokens, :], weight, NT,
                                preferred_element_type=jnp.float32)
 
-    def out_other(s, col):
-        fs = place(s, col)
+    def out_other(n):
+        fs = place(n)
         for kind in ("oa", "ob"):
             ref = view(kind, 0, fs, 1 - c)
             pltpu.make_async_remote_copy(
@@ -460,8 +464,8 @@
             src_ref=psend.at[fs], dst_ref=other_out.at[:, block_cols(fs)], send_sem=psend_sem,
             recv_sem=precv_sem, device_id=partner, device_id_type=MESH).start()
 
-    def out_own(s):
-        zs = nearest(z, s)
+    def out_own(n):
+        zs = picked(n, OWN_ORDER)
         both = pl.ds(zs * 2, 2)
         weight = jnp.concatenate([woa[both].reshape(span, cut),
                                   wob[both].reshape(span, half_out - cut)], axis=1)
@@ -472,9 +476,10 @@
 
     def own_first(i, carry):
         stretches(0, i, Z_LINE)
-        sibling_arrived(("a", "b"), 0, i)
-        normalize(0, nearest(z, i), inv_own)
-        project(0, 0, nearest(z, i))
+        zs = picked(i, FIRST_ORDER)
+        sibling_arrived(("a", "b"), 0, zs)
+        normalize(0, zs, inv_own)
+        project(0, 0, zs)
         return carry
 
     lax.fori_loop(0, Z_LINE, own_first, 0)
@@ -498,17 +503,18 @@
 
     def other_second(i, carry):
         stretches(11, i, Z_LINE)
-        sibling_arrived(("a", "b"), 1, i)
-        project(1, 1, nearest(z, i))
+        zs = picked(i, SECOND_ORDER)
+        sibling_arrived(("a", "b"), 1, zs)
+        project(1, 1, zs)
         return carry
 
     lax.fori_loop(0, Z_LINE, other_second, 0)
     stretch(15)
     attend(1, 1)
     stretch(16)
-    out_other(0, 0)
+    out_other(0)
     stretch(17)
-    out_other(0, 1)
+    out_other(1)
 
     def own_second(i, carry):
         stretches(18, i, Z_LINE)
@@ -517,25 +523,25 @@
 
     lax.fori_loop(0, Z_LINE, own_second, 0)
     stretch(22)
-    out_other(1, 0)
+    out_other(2)
     stretch(23)
-    out_other(1, 1)
+    out_other(3)
     stretch(24)
     attend(1, 0)
     stretch(25)
-    out_other(2, 0)
+    out_other(4)
     stretch(26)
     out_own(0)
     stretch(27)
-    out_other(2, 1)
+    out_other(5)
     stretch(28)
     out_own(1)
     stretch(29)
-    out_other(3, 0)
+    out_other(6)
     stretch(30)
     out_own(2)
     stretch(31)
-    out_other(3, 1)
+    out_other(7)
     stretch(32)
     out_own(3)
     for number in range(33, len(EDGE_PLAN)):

time: 73.5 us -> 70.1 us (0.954)
  Pallas kernels: 72.1 us -> 68.7 us
    pallas_call x1, Pallas kernels: 72.1 us -> 68.7 us  [fused(): pl.pallas_call(block_kernel, out_shape=(jax.ShapeDtypeStruct((tokens, wid...]
where the time goes in v4:
time: 70.1 us; the launch traced here: 70 us
  Pallas kernels  68.7 us (98%)
  other arithmetic  1.26 us (2%)
    pallas_call x1, Pallas kernels, fused(): pl.pallas_call(block_kernel, out_shape=(jax.ShapeDtypeStruct((tokens, wid...  68.7 us

profile of v4, /device:TPU:0, one launch (start us, length us, event | category | flops | bytes accessed | tf_op | source)
XLA Modules:
  0.0 70.0 jit_solution(7501850314826264679)
XLA Ops:
  0.0 68.7 %attention_block.1 = (f32[256,2048]{1,0:T(8,128)S(1)}, bf16[256,2048]{1,0:T(8,128)(2,1)S(1)}) custom-call(bf16[256,2048]{1,0:T(8,128)(2,1)} %hid_hbm.1, bf16[1,64]{1,0:T(2,128)(2,1)} %bitcast.3, bf16[64,2048]{1,0:T(8,128)(2,1)} %wq_hbm.1, bf16[64,512]{1,0:T(8,128)(2,1)} %wk_hbm.1, bf16[64,512]{1,0:T(8,128)(2,1)} %wv_hbm.1, bf16[64,2048]{1,0:T(8,128)(2,1)} %bitcast.2, ...), custom_call_target="tpu_custom_call" | custom-call | tf_op jit(solution)/shard_map/attention_block/pallas_call | solution.py:581
  68.7 1.3 %add_convert_fusion = bf16[256,2048]{1,0:T(8,128)(2,1)} fusion(f32[256,2048]{1,0:T(8,128)S(1)} %get-tuple-element.7, bf16[256,2048]{1,0:T(8,128)(2,1)S(1)} %get-tuple-element.8), kind=kLoop, calls=%fused_computation | loop fusion | flops 1572864 | bytes 4194304 | tf_op jit(solution)/shard_map/convert_element_type | solution.py:619

commit v5 on v4

--- a/solution.py
+++ b/solution.py
@@ -23,37 +23,37 @@
 BUFFERS = ("a", "b", "oa", "ob")
 PIECES = (("a", 0), ("a", 1), ("b", 0), ("b", 1), ("oa", 0), ("ob", 0))
 EDGE_PLAN = (
-    (102, 100, 101, 103, 4, 1, 20, 25, 17,),
-    (18, 104, 28, 12, 2, 21, 5, 3, 9, 6, 22, 19, 23,),
-    (7, 11,),
-    (),
-    (),
-    (10,),
-    (13,),
-    (29, 27, 15,),
-    (),
-    (105, 31,),
-    (26,),
-    (30, 14,),
-    (),
-    (),
-    (),
-    (),
-    (),
-    (33, 41, 36, 44,),
-    (),
-    (),
-    (),
-    (),
-    (),
-    (34, 42, 45,),
-    (37,),
+    (100, 102, 101, 103, 1, 17, 20, 4, 28, 25, 18, 9, 5, 21, 12, 2,),
+    (3, 13, 22, 19, 23, 104, 6, 7, 10,),
+    (),
+    (),
+    (),
+    (11,),
+    (),
+    (29,),
+    (),
+    (),
+    (),
+    (105, 14, 26,),
+    (30, 15, 27,),
+    (31,),
+    (),
+    (),
+    (36,),
+    (44, 33,),
+    (),
+    (),
+    (41,),
+    (),
+    (),
+    (34, 42,),
+    (45, 37,),
     (),
     (),
     (35, 43,),
-    (38,),
+    (38, 47,),
     (46,),
-    (47,),
+    (),
     (39,),
     (),
     (),
@@ -67,36 +67,36 @@
     (),
 )
 MIDDLE_PLAN = (
-    (100, 102, 101, 103, 5, 0, 18, 16, 2, 21, 20, 13, 24, 3, 19,),
-    (4, 22, 8, 6, 23,),
-    (11, 7, 28,),
-    (10, 29, 27,),
-    (31,),
-    (),
-    (15, 12, 26,),
-    (30,),
-    (),
-    (104,),
-    (14, 105,),
-    (),
-    (),
-    (),
-    (),
-    (),
-    (32,),
-    (34, 40, 42,),
-    (),
-    (37,),
-    (),
-    (),
-    (),
-    (44, 45, 35, 43,),
-    (36,),
-    (),
-    (),
-    (),
-    (46,),
-    (38, 47, 39,),
+    (100, 102, 101, 103, 0, 18, 21, 5, 2, 16, 20, 3, 8, 4, 13,),
+    (22, 24, 19, 23, 28, 10, 11, 29, 27, 6, 26,),
+    (7, 31,),
+    (30, 104,),
+    (),
+    (12,),
+    (),
+    (),
+    (14,),
+    (),
+    (105, 15,),
+    (),
+    (),
+    (),
+    (),
+    (34,),
+    (),
+    (42, 32, 37,),
+    (45,),
+    (40,),
+    (),
+    (44,),
+    (),
+    (38,),
+    (35,),
+    (43,),
+    (47, 46,),
+    (36, 39,),
+    (),
+    (),
     (),
     (),
     (),
@@ -110,13 +110,13 @@
     (),
     (),
 )
-FIRST_ORDER = ((0, 2, 1, 3), (1, 0, 3, 2))
-SECOND_ORDER = ((1, 3, 0, 2), (3, 0, 2, 1))
+FIRST_ORDER = ((1, 0, 2, 3), (0, 1, 2, 3))
+SECOND_ORDER = ((1, 0, 2, 3), (0, 2, 1, 3))
 OTHER_ORDER = (
-    ((0, 0), (0, 1), (1, 0), (0, 2), (1, 1), (0, 3), (1, 2), (1, 3)),
-    ((0, 1), (0, 0), (0, 2), (0, 3), (1, 0), (1, 1), (1, 3), (1, 2)),
+    ((0, 0), (1, 0), (0, 1), (0, 2), (1, 1), (0, 3), (1, 2), (1, 3)),
+    ((0, 1), (0, 2), (1, 1), (0, 0), (0, 3), (1, 2), (1, 0), (1, 3)),
 )
-OWN_ORDER = ((0, 1, 2, 3), (0, 1, 3, 2))
+OWN_ORDER = ((0, 1, 2, 3), (1, 2, 0, 3))
 
 
 def rope_tables(tokens, head_dim):

time: 70.1 us -> 70.1 us (level)
  no operation moved by 1% of the time
where the time goes in v5:
time: 70.1 us; the launch traced here: 69.9 us
  Pallas kernels  68.7 us (98%)
  other arithmetic  1.26 us (2%)
    pallas_call x1, Pallas kernels, fused(): pl.pallas_call(block_kernel, out_shape=(jax.ShapeDtypeStruct((tokens, wid...  68.7 us

profile of v5, /device:TPU:0, one launch (start us, length us, event | category | flops | bytes accessed | tf_op | source)
XLA Modules:
  0.0 69.9 jit_solution(10869743295556404642)
XLA Ops:
  0.0 68.7 %attention_block.1 = (f32[256,2048]{1,0:T(8,128)S(1)}, bf16[256,2048]{1,0:T(8,128)(2,1)S(1)}) custom-call(bf16[256,2048]{1,0:T(8,128)(2,1)} %hid_hbm.1, bf16[1,64]{1,0:T(2,128)(2,1)} %bitcast.3, bf16[64,2048]{1,0:T(8,128)(2,1)} %wq_hbm.1, bf16[64,512]{1,0:T(8,128)(2,1)} %wk_hbm.1, bf16[64,512]{1,0:T(8,128)(2,1)} %wv_hbm.1, bf16[64,2048]{1,0:T(8,128)(2,1)} %bitcast.2, ...), custom_call_target="tpu_custom_call" | custom-call | tf_op jit(solution)/shard_map/attention_block/pallas_call | solution.py:581
  68.7 1.3 %add_convert_fusion = bf16[256,2048]{1,0:T(8,128)(2,1)} fusion(f32[256,2048]{1,0:T(8,128)S(1)} %get-tuple-element.7, bf16[256,2048]{1,0:T(8,128)(2,1)S(1)} %get-tuple-element.8), kind=kLoop, calls=%fused_computation | loop fusion | flops 1572864 | bytes 4194304 | tf_op jit(solution)/shard_map/convert_element_type | solution.py:619
